TPU v7x, 256 devices: a whole 4x4x8 slice. The times are simulated.
256 devices in a mesh: atom: 32 (over x, z_lo, core), chan: 8 (over y, z_hi).
Axes of the slice: x: 4, y: 4, z: 8 (z_hi: 2, z_lo: 4; z = z_hi * 4 + z_lo), core: 2. Of those that a mesh axis runs over, the one named last changes fastest.
Arguments:
- positions: float32 [3, 4096], P(None, 'atom'), may hold values from -9 to 9
- features: bfloat16 [512, 4096], P('chan', 'atom'), may hold values from -6 to 6
- struct_ids: int32 [4096], P('atom'), may hold values from 0 to 31, as said below
- slots: int32 [64, 4096], P(None, 'atom'), may hold values from 0 to 96, as said below
- validity: int32 [64, 4096], P(None, 'atom'), may hold values from 0 to 1, as said below
- radial_in: bfloat16 [512, 128], replicated, may hold values from -72 to 72
- radial_out: bfloat16 [512, 512], P('chan'), may hold values from -0.0234375 to 0.0234375
- mixing: bfloat16 [512, 512], P(None, 'chan'), may hold values from -0.5 to 0.5
- readout: float32 [512], replicated, may hold values from -0.0078125 to 0.0078125
Outputs:
- forces: float32 [3, 4096], P(None, 'atom')
- stress: float32 [9, 32], replicated
Inputs may be any that keep to these rules, and one draw needn't show every extreme that they name: `struct_ids`: structure numbers never fall along the atoms and every structure has at least one atom. `slots`: the 64 slot values of one atom are distinct and never equal 48. `validity`: an edge is valid only where its neighbour atom exists and belongs to the same structure.
All inputs are finite; a program needn't handle non-finite values.
Results may differ from a plain program's by a relative error of at most 0.0099.
Values may be sent and summed in bfloat16 or wider, within the bound.
No kernel may reach another device: no remote copies, remote signals or barrier semaphores. Data moves between devices by JAX's collectives and lax.ppermute only.
A program may use at most 64 MiB of HBM per device.

v0:
```python
import jax
import jax.numpy as jnp
from jax import lax
from jax.sharding import PartitionSpec as P

RIM = 48


sharpness = 40.0
reach = 10.0


def with_halo(value, sides, width):
    for axis, dim in sides:
        size, length = (lax.axis_size(axis), value.shape[dim])
        up = [(i, (i + 1) % size) for i in range(size - 1)]
        down = [(j, i) for i, j in up]
        last = lax.slice_in_dim(value, length - width, length, axis=dim)
        first = lax.slice_in_dim(value, 0, width, axis=dim)
        before = lax.ppermute(last, axis, up)
        after = lax.ppermute(first, axis, down)
        value = jnp.concatenate([before, value, after], axis=dim)
    return value


def turned_gather(arrays, axis, dims):
    turned = [jnp.moveaxis(a, dim, 0) for a, dim in zip(arrays, dims)]
    both = jnp.concatenate([t.reshape(len(t), -1) for t in turned], axis=1)
    result, at, outs = (lax.all_gather(both, axis, axis=0, tiled=True), 0, [])
    for t, dim in zip(turned, dims):
        share = result[:, at : at + t[0].size].reshape(-1, *t.shape[1:])
        outs.append(jnp.moveaxis(share, 0, dim))
        at += t[0].size
    return tuple(outs)


def sent_to_all(value, axis):
    copies = jnp.broadcast_to(value, (lax.axis_size(axis), *value.shape))
    return lax.all_to_all(copies, axis, split_axis=0, concat_axis=0, tiled=True)


def of_everyone(value, axis):
    everything = sent_to_all(value, axis)
    return jnp.sum(everything, axis=0)


def packed_total(arrays, axis):
    flat, at, outs = (jnp.concatenate([a.reshape(-1) for a in arrays]), 0, [])
    running = of_everyone(flat, axis)
    for a in arrays:
        outs.append(running[at : at + a.size].reshape(a.shape))
        at += a.size
    return tuple(outs)


def from_behind(value, axis, by):
    size = lax.axis_size(axis)
    pairs = [(i, i + by) for i in range(size) if 0 <= i + by < size]
    return lax.ppermute(value, axis, pairs)


def dsilu(value):
    sigma = jax.nn.sigmoid(value)
    return sigma * (1.0 + value * (1.0 - sigma))


def radial_terms(vector, radial_in, radial_out):
    dist = jnp.sqrt(1.0 + jnp.sum(vector * vector, axis=0))
    count = radial_in.shape[1]
    centers = jnp.arange(count).astype(jnp.float32) * (reach / count)
    offset = dist[None, :] - centers[:, None]
    bump = jnp.exp(-sharpness * offset * offset)
    basis = bump.astype(jnp.bfloat16)
    slope = (-2.0 * sharpness * offset * bump).astype(jnp.bfloat16)
    pre = jnp.dot(radial_in, basis, preferred_element_type=jnp.float32)
    dpre = jnp.dot(radial_in, slope, preferred_element_type=jnp.float32)
    hidden = jax.nn.silu(pre).astype(jnp.bfloat16)
    dhidden = (dsilu(pre) * dpre).astype(jnp.bfloat16)
    radial = jnp.dot(radial_out, hidden, preferred_element_type=jnp.float32)
    dradial = jnp.dot(radial_out, dhidden, preferred_element_type=jnp.float32)
    return (dist, radial, dradial)


def local(positions, features, struct_ids, slots, validity, radial_in, radial_out, mixing, readout):
    slot_count, atom_count = slots.shape
    padded_feat, padded_pos = (
        with_halo(features.astype(jnp.float32), (("atom", 1),), RIM).astype(features.dtype),
        with_halo(positions, (("atom", 1),), RIM),
    )
    atom_index = jnp.arange(atom_count, dtype=jnp.int32)
    whole_feat, whole_radial, whole_mix = turned_gather(
        (padded_feat, radial_out, mixing), "chan", (0, 0, 1)
    )
    used = slot_count // lax.axis_size("chan")
    first = lax.axis_index("chan") * used
    slot_rows = lax.dynamic_slice_in_dim(slots, first, used, 0)
    valid_rows = lax.dynamic_slice_in_dim(validity, first, used, 0)
    flat_index = (atom_index[None, :] + slot_rows).reshape(-1)
    far_feat = whole_feat[:, flat_index]
    vector = padded_pos[:, flat_index] - jnp.tile(positions, (1, used))
    weight = valid_rows.reshape(-1).astype(jnp.float32)
    dist, radial, dradial = radial_terms(vector, radial_in, whole_radial)
    message = (far_feat * radial).astype(jnp.bfloat16)
    mixed = jnp.dot(whole_mix, message, preferred_element_type=jnp.float32)
    gmix = (weight[None, :] * readout[:, None] * dsilu(mixed)).astype(jnp.bfloat16)
    gmsg = lax.dot_general(
        whole_mix, gmix, (((0,), (0,)), ((), ())), preferred_element_type=jnp.float32
    )
    gdist = jnp.sum(gmsg * far_feat.astype(jnp.float32) * dradial, axis=0)
    gvec = gdist * vector / dist
    outgoing = gvec.reshape(3, used, atom_count).sum(axis=1)
    table = jnp.zeros((3, atom_count + 2 * RIM), jnp.float32).at[:, flat_index].add(-gvec)
    table = table.at[:, RIM : RIM + atom_count].add(outgoing)
    atomvir = (vector[:, None, :] * gvec[None, :, :]).reshape(9, used, atom_count).sum(axis=1)
    table, atomvir = packed_total((table, atomvir), "chan")
    from_next = from_behind(table[:, :RIM], "atom", -1)
    from_prior = from_behind(table[:, RIM + atom_count :], "atom", 1)
    forces = table[:, RIM : RIM + atom_count]
    forces = forces + jnp.pad(from_prior, ((0, 0), (0, atom_count - RIM)))
    forces = forces + jnp.pad(from_next, ((0, 0), (atom_count - RIM, 0)))
    struct_total = atom_count * lax.axis_size("atom") // 128
    onehot = (struct_ids[None, :] == jnp.arange(struct_total, dtype=jnp.int32)[:, None]).astype(
        jnp.float32
    )
    virial = jnp.dot(atomvir, onehot.T, precision=lax.Precision.HIGHEST)
    counts = jnp.sum(onehot, axis=1)
    virial, counts = packed_total((virial, counts), "atom")
    stress = -virial / counts[None, :]
    return (forces, stress)


def solution(mesh):
    placed = (
        P(None, "atom"),
        P("chan", "atom"),
        P("atom"),
        P(None, "atom"),
        P(None, "atom"),
        P(),
        P("chan", None),
        P(None, "chan"),
        P(),
    )
    return jax.shard_map(
        local, mesh=mesh, in_specs=placed, out_specs=(P(None, "atom"), P()), check_vma=False
    )
```

profile of v0, /device:TPU:1, one launch (start us, length us, event | category | flops | bytes accessed | tf_op | source)
XLA Modules:
  0.0 156.5 jit_solution(10200751247860224397)
XLA Ops:
  7.2 0.9 fusion.56
  8.1 4.9 %collective-permute-start = (bf16[64,48]{1,0:T(8,128)(2,1)S(1)}, bf16[64,48]{1,0:T(8,128)(2,1)S(1)}, u32[]{:S(2)}, u32[]{:S(2)}) collective-permute-start(bf16[64,48]{1,0:T(8,128)(2,1)S(1)} %get-tuple-element.19), channel_id=1, source_target_pairs={{0,8},{8,16},{16,24},{24,32},{32,40},{40,48},{48,56},{56,64},{64,7... | collective-permute-start | bytes 18440 | tf_op jit(solution)/shard_map/ppermute | solution.py:20
  13.0 1.9 %collective-permute-start.1 = (bf16[64,48]{1,0:T(8,128)(2,1)S(1)}, bf16[64,48]{1,0:T(8,128)(2,1)S(1)}, u32[]{:S(2)}, u32[]{:S(2)}) collective-permute-start(bf16[64,48]{1,0:T(8,128)(2,1)S(1)} %get-tuple-element.18), channel_id=1, source_target_pairs={{8,0},{16,8},{24,16},{32,24},{40,32},{48,40},{56,48},{64,56},{72,6... | collective-permute-start | bytes 18440 | tf_op jit(solution)/shard_map/ppermute | solution.py:21
  15.0 3.1 %collective-permute-done.1 = bf16[64,48]{1,0:T(8,128)(2,1)S(1)} collective-permute-done((bf16[64,48]{1,0:T(8,128)(2,1)S(1)}, bf16[64,48]{1,0:T(8,128)(2,1)S(1)}, u32[]{:S(2)}, u32[]{:S(2)}) %collective-permute-start.1) | collective-permute-done | bytes 6176 | tf_op jit(solution)/shard_map/ppermute | solution.py:21
  18.1 1.7 %concatenate.17 = bf16[64,1248]{1,0:T(8,128)(2,1)} concatenate(bf16[64,48]{1,0:T(8,128)(2,1)S(1)} %collective-permute-done, bf16[64,128]{1,0:T(8,128)(2,1)} %param.12, bf16[64,48]{1,0:T(8,128)(2,1)S(1)} %collective-permute-done.1, bf16[64,512]{1,0:T(8,128)(2,1)} %param.17, bf16[64,512]{1,0:T(8,128)(2,1)} %bitcast.80), dimensions={1} | concatenate | bytes 319488 | tf_op jit(solution)/shard_map/concatenate | solution.py:28
  19.8 0.8 fusion.58
  20.6 1.9 %collective-permute-start.3 = (f32[3,48]{1,0:T(4,128)S(1)}, f32[3,48]{1,0:T(4,128)S(1)}, u32[]{:S(2)}, u32[]{:S(2)}) collective-permute-start(f32[3,48]{1,0:T(4,128)S(1)} %get-tuple-element.25), channel_id=1, source_target_pairs={{8,0},{16,8},{24,16},{32,24},{40,32},{48,40},{56,48},{64,56},{72,6... | collective-permute-start | bytes 1736 | tf_op jit(solution)/shard_map/ppermute | solution.py:21
  22.6 3.6 %collective-permute-start.2 = (f32[3,48]{1,0:T(4,128)S(1)}, f32[3,48]{1,0:T(4,128)S(1)}, u32[]{:S(2)}, u32[]{:S(2)}) collective-permute-start(f32[3,48]{1,0:T(4,128)S(1)} %get-tuple-element.24), channel_id=1, source_target_pairs={{0,8},{8,16},{16,24},{24,32},{32,40},{40,48},{48,56},{56,64},{64,7... | collective-permute-start | bytes 1736 | tf_op jit(solution)/shard_map/ppermute | solution.py:20
  26.2 0.7 dynamic-slice_add_fusion
  26.9 1.3 convert_bitcast_fusion
  28.2 0.7 broadcast_bitcast_fusion
  28.9 0.7 compare_reduce_fusion
  29.6 0.8 pad_maximum_fusion.1
  30.4 0.1 copy.79
  30.5 2.8 %gather_fusion.1 = f32[1024,3]{1,0:T(8,128)S(1)} fusion(f32[3,224]{0,1:T(8,128)S(1)} %copy.79, s32[1024]{0:T(1024)S(1)} %broadcast_clamp_fusion), kind=kCustom, calls=%fused_computation.1 | custom fusion | bytes 28672 | tf_op jit(solution)/shard_map/gather | solution.py:100
  33.3 0.2 copy.80
  33.6 0.5 fusion.25
  34.2 52.5 %all-gather.2.cloned.1.call-done = bf16[512,1248]{1,0:T(8,128)(2,1)} async-done(((bf16[64,1248]{1,0:T(8,128)(2,1)}), bf16[512,1248]{1,0:T(8,128)(2,1)}) %all-gather.2.cloned.1.call-update) | async-done | bytes 1277968 | tf_op jit(solution)/shard_map/all_gather | solution.py:29
  86.7 1.0 slice.91
  87.7 0.1 copy.91
  87.8 4.0 %gather_fusion = bf16[1024,512]{1,0:T(8,128)(2,1)S(1)} fusion(bf16[512,224]{0,1:T(8,128)(2,1)S(1)} %copy.91, s32[1024]{0:T(1024)S(1)} %broadcast_clamp_fusion), kind=kCustom, calls=%fused_computation | custom fusion | bytes 2101248 | tf_op jit(solution)/shard_map/gather | solution.py:99
  91.8 1.3 copy.78
  93.1 3.6 %multiply_convert_fusion = bf16[512,1024]{0,1:T(8,128)(2,1)S(1)} fusion(bf16[1024,512]{0,1:T(8,128)(2,1)} %copy.78, f32[1024,512]{1,0:T(8,128)S(1)} %fusion.25, f32[512]{0:T(512)S(1)} %copy-done.7, f32[1024]{0:T(1024)S(1)} %copy-done.3, bf16[512,1248]{1,0:T(8,128)(2,1)} %all-gather.2.cloned.1.call-done), kind=kOutput, calls=%fused_computation.19 | convolution fusion | flops 1083179008 | bytes 5249024 | tf_op jit(solution)/shard_map/dot_general | solution.py:104
  96.8 1.9 %fusion.20 = f32[512,1024]{1,0:T(8,128)S(1)} fusion(bf16[512,1024]{0,1:T(8,128)(2,1)S(1)} %multiply_convert_fusion, bf16[512,1248]{1,0:T(8,128)(2,1)} %all-gather.2.cloned.1.call-done), kind=kOutput, calls=%fused_computation.30 | convolution fusion | flops 536870912 | bytes 3670016 | tf_op jit(solution)/shard_map/dot_general | solution.py:106
  98.7 3.5 %fusion.9 = f32[1024]{0:T(1024)S(1)} fusion(f32[512,1024]{1,0:T(8,128)S(1)} %fusion.20, bf16[1024,512]{0,1:T(8,128)(2,1)} %copy.78, f32[1024,512]{1,0:T(8,128)} %copy-done.1, bf16[512,128]{1,0:T(8,128)(2,1)S(1)} %copy-done, bf16[512,1248]{1,0:T(8,128)(2,1)} %all-gather.2.cloned.1.call-done, f32[128]{0:T(128)S(1)} %copy-done.5, f32[1024]{0:T(1024)S(1)} %get-tuple-element.23), kind=kOutput, calls=%fused_computation.18 | convolution fusion | flops 678689792 | bytes 5906944 | tf_op jit(solution)/shard_map/dot_general | solution.py:80
  102.3 0.2 copy.83
  102.5 6.0 %scatter_custom_fusion = f32[3,224]{0,1:T(8,128)S(1)} fusion(s32[1024]{0:T(1024)S(1)} %bitcast.84, f32[1024,3]{1,0:T(8,128)S(1)} %copy.83, f32[]{:T(128)} %constant.45.clone.1), kind=kCustom, calls=%fused_computation.43 | custom fusion | flops 3072 | bytes 2692 | tf_op jit(solution)/shard_map/scatter-add | solution.py:112
  108.6 0.1 copy.84
  108.7 0.7 fusion.38
  109.5 0.1 reshape.205
  109.6 0.1 pad_maximum_fusion
  109.7 0.7 broadcast_in_dim.7
  110.3 3.7 %all-to-all-start = ((f32[8,1,1824]{2,1,0:T(1,128)}), f32[8,1,1824]{2,1,0:T(1,128)S(1)}, u32[]{:S(2)}, u32[]{:S(2)}) async-start(f32[8,1,1824]{2,1,0:T(1,128)} %broadcast_in_dim.7), calls=%async_computation | async-start | bytes 122880 | tf_op jit(solution)/shard_map/all_to_all | solution.py:39
  114.1 0.1 convert_reduce_fusion
  114.2 9.0 %all-to-all-done = f32[8,1,1824]{2,1,0:T(1,128)S(1)} async-done(((f32[8,1,1824]{2,1,0:T(1,128)}), f32[8,1,1824]{2,1,0:T(1,128)S(1)}, u32[]{:S(2)}, u32[]{:S(2)}) %all-to-all-start) | async-done | bytes 58400 | tf_op jit(solution)/shard_map/all_to_all | solution.py:39
  123.2 0.2 fusion.41
  123.4 0.1 reshape.207
  123.5 0.1 fusion.57
  123.6 6.9 %collective-permute-start.5 = (f32[3,48]{1,0:T(4,128)S(1)}, f32[3,48]{1,0:T(4,128)S(1)}, u32[]{:S(2)}, u32[]{:S(2)}) collective-permute-start(f32[3,48]{1,0:T(4,128)S(1)} %get-tuple-element.21), channel_id=1, source_target_pairs={{8,0},{16,8},{24,16},{32,24},{40,32},{48,40},{56,48},{64,56},{72,6... | collective-permute-start | bytes 1736 | tf_op jit(solution)/shard_map/ppermute | solution.py:59
  130.4 2.6 %collective-permute-start.4 = (f32[3,48]{1,0:T(4,128)S(1)}, f32[3,48]{1,0:T(4,128)S(1)}, u32[]{:S(2)}, u32[]{:S(2)}) collective-permute-start(f32[3,48]{1,0:T(4,128)S(1)} %get-tuple-element.20), channel_id=1, source_target_pairs={{0,8},{8,16},{16,24},{24,32},{32,40},{40,48},{48,56},{56,64},{64,7... | collective-permute-start | bytes 1736 | tf_op jit(solution)/shard_map/ppermute | solution.py:59
  133.0 0.1 reshape.209
  133.1 0.1 pad_maximum_fusion.2
  133.2 0.6 broadcast_in_dim.8
  133.8 7.3 %all-to-all-start.1 = ((f32[32,1,320]{2,1,0:T(1,128)}), f32[32,1,320]{2,1,0:T(1,128)S(1)}, u32[]{:S(2)}, u32[]{:S(2)}) async-start(f32[32,1,320]{2,1,0:T(1,128)} %broadcast_in_dim.8), calls=%async_computation.1 | async-start | bytes 98304 | tf_op jit(solution)/shard_map/all_to_all | solution.py:39
  141.2 0.7 fusion.46
  141.9 7.0 %all-to-all-done.1 = f32[32,1,320]{2,1,0:T(1,128)S(1)} async-done(((f32[32,1,320]{2,1,0:T(1,128)}), f32[32,1,320]{2,1,0:T(1,128)S(1)}, u32[]{:S(2)}, u32[]{:S(2)}) %all-to-all-start.1) | async-done | bytes 40992 | tf_op jit(solution)/shard_map/all_to_all | solution.py:39
  149.0 0.1 neg.21
  149.1 0.6 broadcast_divide_fusion
  (39 shorter events, 0.5 us)
Async XLA Ops:
  7.2 26.4 %copy-start = (bf16[512,128]{1,0:T(8,128)(2,1)S(1)}, bf16[512,128]{1,0:T(8,128)(2,1)}, u32[]{:S(2)}) copy-start(bf16[512,128]{1,0:T(8,128)(2,1)} %param.16) | copy-start | bytes 393220
  7.2 79.5 %all-gather.2.cloned.1.call-start = ((), (), s32[]{:S(2)}) async-start(), calls=%async_computation.2 | async-start | bytes 1474560 | tf_op jit(solution)/shard_map/all_gather | solution.py:29
  8.1 6.9 %collective-permute-start = (bf16[64,48]{1,0:T(8,128)(2,1)S(1)}, bf16[64,48]{1,0:T(8,128)(2,1)S(1)}, u32[]{:S(2)}, u32[]{:S(2)}) collective-permute-start(bf16[64,48]{1,0:T(8,128)(2,1)S(1)} %get-tuple-element.19), channel_id=1, source_target_pairs={{0,8},{8,16},{16,24},{24,32},{32,40},{40,48},{48,56},{56,64},{64,7... | collective-permute-start | bytes 18440 | tf_op jit(solution)/shard_map/ppermute | solution.py:20
  13.0 5.1 %collective-permute-start.1 = (bf16[64,48]{1,0:T(8,128)(2,1)S(1)}, bf16[64,48]{1,0:T(8,128)(2,1)S(1)}, u32[]{:S(2)}, u32[]{:S(2)}) collective-permute-start(bf16[64,48]{1,0:T(8,128)(2,1)S(1)} %get-tuple-element.18), channel_id=1, source_target_pairs={{8,0},{16,8},{24,16},{32,24},{40,32},{48,40},{56,48},{64,56},{72,6... | collective-permute-start | bytes 18440 | tf_op jit(solution)/shard_map/ppermute | solution.py:21
  20.6 9.0 %collective-permute-start.3 = (f32[3,48]{1,0:T(4,128)S(1)}, f32[3,48]{1,0:T(4,128)S(1)}, u32[]{:S(2)}, u32[]{:S(2)}) collective-permute-start(f32[3,48]{1,0:T(4,128)S(1)} %get-tuple-element.25), channel_id=1, source_target_pairs={{8,0},{16,8},{24,16},{32,24},{40,32},{48,40},{56,48},{64,56},{72,6... | collective-permute-start | bytes 1736 | tf_op jit(solution)/shard_map/ppermute | solution.py:21
  22.6 7.1 %collective-permute-start.2 = (f32[3,48]{1,0:T(4,128)S(1)}, f32[3,48]{1,0:T(4,128)S(1)}, u32[]{:S(2)}, u32[]{:S(2)}) collective-permute-start(f32[3,48]{1,0:T(4,128)S(1)} %get-tuple-element.24), channel_id=1, source_target_pairs={{0,8},{8,16},{16,24},{24,32},{32,40},{40,48},{48,56},{56,64},{64,7... | collective-permute-start | bytes 1736 | tf_op jit(solution)/shard_map/ppermute | solution.py:20
  28.9 5.2 %copy-start.4 = (f32[128]{0:T(128)}, f32[128]{0:T(128)S(1)}, u32[]{:S(2)}) copy-start(f32[128]{0:T(128)S(1)} %convert_multiply_fusion) | copy-start | bytes 1540
  34.1 59.0 %copy-start.1 = (f32[1024,512]{1,0:T(8,128)}, f32[1024,512]{1,0:T(8,128)S(1)}, u32[]{:S(2)}) copy-start(f32[1024,512]{1,0:T(8,128)S(1)} %fusion.25) | copy-start | bytes 6291460
  91.8 1.4 copy-start.3
  91.8 1.4 copy-start.7
  96.8 1.9 %copy-start.5 = (f32[128]{0:T(128)S(1)}, f32[128]{0:T(128)}, u32[]{:S(2)}) copy-start(f32[128]{0:T(128)} %copy-done.4) | copy-start | bytes 1540
  98.7 9.9 %copy-start.2 = (f32[3,128]{1,0:T(4,128)S(1)}, f32[3,128]{1,0:T(4,128)}, u32[]{:S(2)}) copy-start(f32[3,128]{1,0:T(4,128)} %param.11) | copy-start | bytes 4612
  98.7 15.4 %copy-start.6 = (s32[128]{0:T(128)S(1)}, s32[128]{0:T(128)}, u32[]{:S(2)}) copy-start(s32[128]{0:T(128)} %param.13) | copy-start | bytes 1540
  110.3 12.8 %all-to-all-start = ((f32[8,1,1824]{2,1,0:T(1,128)}), f32[8,1,1824]{2,1,0:T(1,128)S(1)}, u32[]{:S(2)}, u32[]{:S(2)}) async-start(f32[8,1,1824]{2,1,0:T(1,128)} %broadcast_in_dim.7), calls=%async_computation | async-start | bytes 122880 | tf_op jit(solution)/shard_map/all_to_all | solution.py:39
  123.6 17.6 %collective-permute-start.5 = (f32[3,48]{1,0:T(4,128)S(1)}, f32[3,48]{1,0:T(4,128)S(1)}, u32[]{:S(2)}, u32[]{:S(2)}) collective-permute-start(f32[3,48]{1,0:T(4,128)S(1)} %get-tuple-element.21), channel_id=1, source_target_pairs={{8,0},{16,8},{24,16},{32,24},{40,32},{48,40},{56,48},{64,56},{72,6... | collective-permute-start | bytes 1736 | tf_op jit(solution)/shard_map/ppermute | solution.py:59
  130.4 10.8 %collective-permute-start.4 = (f32[3,48]{1,0:T(4,128)S(1)}, f32[3,48]{1,0:T(4,128)S(1)}, u32[]{:S(2)}, u32[]{:S(2)}) collective-permute-start(f32[3,48]{1,0:T(4,128)S(1)} %get-tuple-element.20), channel_id=1, source_target_pairs={{0,8},{8,16},{16,24},{24,32},{32,40},{40,48},{48,56},{56,64},{64,7... | collective-permute-start | bytes 1736 | tf_op jit(solution)/shard_map/ppermute | solution.py:59
  133.8 15.0 %all-to-all-start.1 = ((f32[32,1,320]{2,1,0:T(1,128)}), f32[32,1,320]{2,1,0:T(1,128)S(1)}, u32[]{:S(2)}, u32[]{:S(2)}) async-start(f32[32,1,320]{2,1,0:T(1,128)} %broadcast_in_dim.8), calls=%async_computation.1 | async-start | bytes 98304 | tf_op jit(solution)/shard_map/all_to_all | solution.py:39
Sparse Core Ops, SparseCore 0:
  19.9 66.7 all-gather.1
where the time goes:
time: 157 us
  waiting for transfers between devices  71.6 us (46%)
  starting transfers between devices  32.9 us (21%)
  local copies, waits for them, and re-layouts  15.9 us (10%)
  between operations  14.4 us (9%)
  other arithmetic  12 us (8%)
  matrix products  9.72 us (6%)
    all_gather x1, waiting for transfers between devices, turned_gather(): result, at, outs = (lax.all_gather(both, axis, axis=0, tiled=True), 0, [])  52.5 us
    all_to_all x2, waiting for transfers between devices, sent_to_all(): return lax.all_to_all(copies, axis, split_axis=0, concat_axis=0, tiled=True)  16 us
    all_to_all x2, starting transfers between devices, sent_to_all(): return lax.all_to_all(copies, axis, split_axis=0, concat_axis=0, tiled=True)  11.1 us
    ppermute x2, starting transfers between devices, from_behind(): return lax.ppermute(value, axis, pairs)  9.46 us
    ppermute x2, starting transfers between devices, with_halo(): before = lax.ppermute(last, axis, up)  8.56 us
    scatter-add x1, other arithmetic, local(): jnp.zeros((3, atom_count + 2 * RIM), jnp.float32).at[:, flat_index]  6.03 us
    gather x2, local copies, waits for them, and re-layouts, local(): far_feat = whole_feat[:, flat_index]  5.3 us
    ppermute x2, starting transfers between devices, with_halo(): after = lax.ppermute(first, axis, down)  3.83 us
  transfers between devices with their start and end apart: 9, of which 4 were waited for; matrix products, arithmetic and copies ran while one was open for 7% of the time, Pallas kernels for 0%

commit v1 on v0

v1 whole, which is shorter than its diff:
```python
import functools

import jax
import jax.numpy as jnp
from jax import lax
from jax.experimental import pallas as pl
from jax.experimental.pallas import tpu as pltpu
from jax.sharding import Mesh
from jax.sharding import PartitionSpec as P

RIM = 48
LANES = 128
CHUNK = 256
SHARPNESS = 40.0
REACH = 10.0
STRUCTS = 32

VMEM = pl.BlockSpec(memory_space=pltpu.VMEM)
SMEM = pl.BlockSpec(memory_space=pltpu.SMEM)
F32 = jnp.float32
BF16 = jnp.bfloat16


def iota(shape, dim):
    return lax.broadcasted_iota(jnp.int32, shape, dim)


def dot(a, b):
    return jnp.dot(a, b, preferred_element_type=F32)


def dot_t(a, b):
    return lax.dot_general(a, b, (((1,), (1,)), ((), ())), preferred_element_type=F32)


def sigmoid(v):
    return 0.5 + 0.5 * jnp.tanh(0.5 * v)


def pack_kernel(place, feat, rout, mixt, out):
    chans, rows, width = out.shape
    core = place[2]

    @pl.when(core == 0)
    def _():
        for c in range(chans):
            out[c, :, LANES:] = rout[...]

    @pl.when(core != 0)
    def _():
        for c in range(chans):
            out[c, :, LANES:] = mixt[...]

    for c in range(chans):
        out[c, :, :LANES] = feat[...]


def halo_of(core, sib, cross, lane):
    low = jnp.where(core == 0, sib, cross)
    high = jnp.where(core == 0, cross, sib)
    return jnp.where(lane < 64, low, high)


def slot_index(place, slots):
    used = 8
    first = pl.multiple_of(place[3] * used, used)
    rows = slots[pl.ds(first, used), :]
    return (rows + iota(rows.shape, 1) - RIM) & 255


def stage_kernel(place, pos, sib, cross, slots, radial_in, hidden, dhidden, geo):
    core = place[2]
    idx = slot_index(place, slots)
    lane = iota(idx.shape, 1)
    inner = idx & 127
    vecs = []
    for p in range(3):
        own = jnp.broadcast_to(pos[p : p + 1, :], idx.shape)
        ring = halo_of(
            core,
            jnp.broadcast_to(sib[p : p + 1, :], idx.shape),
            jnp.broadcast_to(cross[p : p + 1, :], idx.shape),
            lane,
        )
        far = jnp.where(
            idx < 128,
            jnp.take_along_axis(own, inner, axis=1),
            jnp.take_along_axis(ring, inner, axis=1),
        )
        vecs.append(far - own)
    dist = jnp.sqrt(1.0 + (vecs[0] * vecs[0] + vecs[1] * vecs[1] + vecs[2] * vecs[2]))
    for p in range(3):
        geo[p] = vecs[p]
    geo[3] = dist
    count = radial_in.shape[1]
    centers = iota((count, LANES), 0).astype(F32) * (REACH / count)
    weights = radial_in[...]
    for k in range(8):
        offset = jnp.broadcast_to(dist[k : k + 1, :], (count, LANES)) - centers
        bump = jnp.exp(-SHARPNESS * offset * offset)
        slope = (-2.0 * SHARPNESS * offset * bump).astype(BF16)
        both = jnp.concatenate([bump.astype(BF16), slope], axis=1)
        pre2 = dot(weights, both)
        pre, dpre = pre2[:, :LANES], pre2[:, LANES:]
        sig = sigmoid(pre)
        silu = pre * sig
        at = slice(k * LANES, (k + 1) * LANES)
        hidden[:, at] = silu.astype(BF16)
        dhidden[:, at] = ((sig + silu * (1.0 - sig)) * dpre).astype(BF16)


def main_kernel(
    place, gathered, swapped, cross, hidden, dhidden, geo, slots, valid, ids, readout, out, table_f, w_rad, w_mixt, w_mix, scale
):
    core = place[2]
    channels = table_f.shape[0]

    def keep(ref, w_ref):
        w_ref[...] = ref[:, :, LANES:].reshape(channels, channels)

    @pl.when(core == 0)
    def _():
        keep(gathered, w_rad)
        keep(swapped, w_mixt)

    @pl.when(core != 0)
    def _():
        keep(swapped, w_rad)
        keep(gathered, w_mixt)

    w_mix[...] = w_mixt[...].T
    lane = iota((channels, LANES), 1)
    own_f = gathered[:, :, :LANES].reshape(channels, LANES)
    sib_f = swapped[:, :, :LANES].reshape(channels, LANES)
    cross_f = cross[...].reshape(channels, LANES)
    table_f[:, :LANES] = own_f
    table_f[:, LANES:] = halo_of(core, sib_f, cross_f, lane)
    turned = jnp.concatenate([readout[...]] * 2, axis=0).T
    for j in range(4):
        scale[j * LANES : (j + 1) * LANES, :] = jnp.broadcast_to(turned[:, j : j + 1], (LANES, LANES))

    idx = slot_index(place, slots)
    first = pl.multiple_of(place[3] * 8, 8)
    weight = valid[pl.ds(first, 8), :].astype(F32)
    gdists = []
    onehots = []
    for n in range(1024 // CHUNK):
        per = CHUNK // LANES
        row_of = iota((256, LANES), 0)
        onehot = jnp.concatenate(
            [
                (row_of == jnp.broadcast_to(idx[k : k + 1, :], (256, LANES))).astype(F32).astype(BF16)
                for k in range(n * per, (n + 1) * per)
            ],
            axis=1,
        )
        onehots.append(onehot)
        at = slice(n * CHUNK, (n + 1) * CHUNK)
        far = dot(table_f[...], onehot)
        radial = dot(w_rad[...], hidden[:, at])
        message = (far * radial).astype(BF16)
        mixed = dot(w_mix[...], message)
        sig = sigmoid(mixed)
        slope = sig + mixed * sig * (1.0 - sig)
        wide = jnp.concatenate([scale[...]] * per, axis=1)
        gmix = (wide * slope).astype(BF16)
        gmsg = dot(w_mixt[...], gmix)
        dradial = dot(w_rad[...], dhidden[:, at])
        gdists.append(jnp.sum(gmsg * far * dradial, axis=0, keepdims=True))
    row8 = iota((8, LANES), 0)
    gdist = jnp.zeros((8, LANES), F32)
    for k in range(8):
        per = CHUNK // LANES
        part = gdists[k // per][:, (k % per) * LANES : (k % per + 1) * LANES]
        gdist = jnp.where(row8 == k, jnp.broadcast_to(part, (8, LANES)), gdist)
    over = gdist * weight / geo[3]
    vecs = [geo[p] for p in range(3)]
    gvec = [over * v for v in vecs]

    def total(v):
        return jnp.broadcast_to(jnp.sum(v, axis=0, keepdims=True), (8, LANES))

    zero = jnp.zeros((8, LANES), F32)
    acc = jnp.zeros((8, 256), F32)
    for k in range(8):
        rows = zero
        for p in range(3):
            rows = jnp.where(row8 == p, jnp.broadcast_to(gvec[p][k : k + 1, :], (8, LANES)), rows)
        per = CHUNK // LANES
        hot = onehots[k // per][:, (k % per) * LANES : (k % per + 1) * LANES]
        rest = rows
        for _ in range(3):
            part = rest.astype(BF16)
            acc = acc + dot_t(part, hot)
            rest = rest - part.astype(F32)
    own, ring = -acc[:, :LANES], -acc[:, LANES:]
    for p in range(3):
        own = own + jnp.where(row8 == p, total(gvec[p]), 0.0)
    pairs = ((0, 0), (0, 1), (0, 2), (1, 1), (1, 2), (2, 2))
    vir = jnp.where(row8 == 6, 1.0, zero)
    for j, (p, q) in enumerate(pairs):
        vir = jnp.where(row8 == j, total(vecs[p] * gvec[q]), vir)
    struct = iota((LANES, LANES), 0) & (STRUCTS - 1)
    member = (struct == jnp.broadcast_to(ids[...], (LANES, LANES))).astype(F32).astype(BF16)
    spread = jnp.zeros((8, LANES), F32)
    rest = vir
    for _ in range(3):
        part = rest.astype(BF16)
        spread = spread + dot_t(part, member)
        rest = rest - part.astype(F32)
    lane8 = iota((8, LANES), 1)
    picked = jnp.where((lane8 >> 5) == (row8 & 3), spread, 0.0)
    first_row = total(jnp.where(row8 < 4, picked, 0.0))
    second_row = total(jnp.where(row8 >= 4, picked, 0.0))
    ring = pltpu.roll(ring, 3, 0)
    result = jnp.where(row8 < 3, own, jnp.where(row8 < 6, ring, jnp.where(row8 == 6, first_row, second_row)))
    for c in range(out.shape[0]):
        out[c] = result


def middle_kernel(place, got, out):
    x, zl, core, nx = place[0], place[1], place[2], 4
    row8, lane8 = iota((8, LANES), 0), iota((8, LANES), 1)
    edge = jnp.where(core == 0, jnp.where(zl == 3, -1, 0), jnp.where(zl == 0, 1, 0))
    source = x + edge
    inside = jnp.logical_and(source >= 0, source < nx)
    source = jnp.clip(source, 0, nx - 1)
    whole = got[0]
    for i in range(1, got.shape[0]):
        whole = whole + got[i]

    def over_y(xx, kk):
        v = got[xx * 8 + kk]
        for y in range(1, 4):
            v = v + got[xx * 8 + y * 2 + kk]
        return v

    mine = over_y(x, core)
    near = pltpu.roll(over_y(x, 1 - core), 5, 0)
    far = over_y(source, 1 - core)
    far = jnp.where(inside, far, 0.0)
    low = lane8 < 64
    is_first = core == 0
    near_mask = jnp.logical_xor(low, is_first)
    mine = mine + jnp.where(near_mask, near, 0.0)
    far = jnp.where(near_mask, 0.0, far)
    result = jnp.where(row8 < 3, mine, jnp.where(row8 < 6, far, whole))
    for c in range(out.shape[0]):
        out[c] = result


def final_kernel(place, got, forces, stress):
    zl, core = place[1], place[2]
    whole = got[0]
    for i in range(1, got.shape[0]):
        whole = whole + got[i]
    mine = got[zl * 2] + got[zl * 2 + 1]
    other = (zl + jnp.where(core == 0, 3, 1)) & 3
    ring = got[other * 2] + got[other * 2 + 1]
    forces[...] = mine[:3, :] + ring[3:6, :]
    count = whole[7:8, 64:96] * 0.125
    where_is = {(0, 0): 0, (0, 1): 1, (0, 2): 2, (1, 1): 3, (1, 2): 4, (2, 2): 5}
    for p in range(3):
        for q in range(3):
            j = where_is[(min(p, q), max(p, q))]
            value = whole[6 + j // 4 : 7 + j // 4, (j % 4) * 32 : (j % 4) * 32 + 32]
            stress[3 * p + q : 3 * p + q + 1, :] = -value / count


def local(positions, features, struct_ids, slots, validity, radial_in, radial_out, mixing, readout):
    place = jnp.stack(
        [
            lax.axis_index("x"),
            lax.axis_index("zl"),
            lax.axis_index("k"),
            lax.axis_index(("y", "zh")),
        ]
    ).astype(jnp.int32)
    atoms = ("x", "zl", "k")
    domains = lax.axis_size(atoms)
    siblings = [(d, d ^ 1) for d in range(domains)]
    crossing = [(d, d + 1) for d in range(1, domains - 1, 2)]
    crossing = crossing + [(j, i) for i, j in crossing]
    channels = readout.shape[0]
    packed = pl.pallas_call(
        pack_kernel,
        out_shape=jax.ShapeDtypeStruct((8, features.shape[0], LANES + channels), BF16),
        in_specs=[SMEM, VMEM, VMEM, VMEM],
        out_specs=VMEM,
        name="pack",
    )(place, features, radial_out, mixing.T)
    gathered = lax.all_to_all(packed, ("y", "zh"), 0, 0, tiled=True)
    pos_sib = lax.ppermute(positions, atoms, siblings)
    pos_cross = lax.ppermute(positions, atoms, crossing)
    edges = 8 * LANES
    hidden, dhidden, geo = pl.pallas_call(
        stage_kernel,
        out_shape=(
            jax.ShapeDtypeStruct((channels, edges), BF16),
            jax.ShapeDtypeStruct((channels, edges), BF16),
            jax.ShapeDtypeStruct((4, 8, LANES), F32),
        ),
        in_specs=[SMEM] + [VMEM] * 5,
        out_specs=(VMEM, VMEM, VMEM),
        cost_estimate=pl.CostEstimate(flops=5_000_000_000, bytes_accessed=4_000_000, transcendentals=1_000_000),
        name="stage",
    )(place, positions, pos_sib, pos_cross, slots, radial_in)
    swapped = lax.ppermute(gathered, atoms, siblings)
    cross = lax.ppermute(gathered[:, :, :LANES], atoms, crossing)
    message = pl.pallas_call(
        main_kernel,
        out_shape=jax.ShapeDtypeStruct((32, 8, LANES), F32),
        in_specs=[SMEM] + [VMEM] * 10,
        out_specs=VMEM,
        scratch_shapes=[
            pltpu.VMEM((channels, 2 * LANES), BF16),
            pltpu.VMEM((channels, channels), BF16),
            pltpu.VMEM((channels, channels), BF16),
            pltpu.VMEM((channels, channels), BF16),
            pltpu.VMEM((channels, LANES), F32),
        ],
        name="main",
    )(
        place,
        gathered,
        swapped,
        cross,
        hidden,
        dhidden,
        geo,
        slots,
        validity,
        struct_ids.reshape(1, LANES),
        readout.reshape(4, LANES),
    )
    got = lax.all_to_all(message, ("x", "y", "k"), 0, 0, tiled=True)
    message = pl.pallas_call(
        middle_kernel,
        out_shape=jax.ShapeDtypeStruct((8, 8, LANES), F32),
        in_specs=[SMEM, VMEM],
        out_specs=VMEM,
        name="middle",
    )(place, got)
    got = lax.all_to_all(message, ("zl", "zh"), 0, 0, tiled=True)
    return pl.pallas_call(
        final_kernel,
        out_shape=(
            jax.ShapeDtypeStruct((3, LANES), F32),
            jax.ShapeDtypeStruct((9, STRUCTS), F32),
        ),
        in_specs=[SMEM, VMEM],
        out_specs=(VMEM, VMEM),
        name="final",
    )(place, got)


def solution(mesh):
    fine = Mesh(mesh.devices.reshape(4, 4, 2, 4, 2), ("x", "zl", "k", "y", "zh"))
    atoms, chans = ("x", "zl", "k"), ("y", "zh")
    placed = (
        P(None, atoms),
        P(chans, atoms),
        P(atoms),
        P(None, atoms),
        P(None, atoms),
        P(),
        P(chans, None),
        P(None, chans),
        P(),
    )
    return jax.shard_map(
        local, mesh=fine, in_specs=placed, out_specs=(P(None, atoms), P()), check_vma=False
    )
```

time: 157 us -> 84.4 us (0.54)
  waiting for transfers between devices: 71.6 us -> 0.01 us
  blocking collectives: 0 us -> 52 us
  starting transfers between devices: 32.9 us -> 12.7 us
  Pallas kernels: 0 us -> 15.8 us
  local copies, waits for them, and re-layouts: 15.9 us -> 2.07 us
  between operations: 14.4 us -> 0.72 us
  other arithmetic: 12 us -> 0.61 us
  matrix products: 9.72 us -> 0 us
    all_gather x1 -> x0, waiting for transfers between devices: 52.5 us -> none  [turned_gather(): result, at, outs = (lax.all_gather(both, axis, axis=0, tiled=True), 0, [])]
    all_to_all x0 -> x3, blocking collectives: none -> 52 us  [the longest x1 27.5 us: local(): gathered = lax.all_to_all(packed, ('y', 'zh'), 0, 0, tiled=True)]
    all_to_all x2 -> x0, waiting for transfers between devices: 16 us -> none  [sent_to_all(): return lax.all_to_all(copies, axis, split_axis=0, concat_axis=0, tiled=True)]
    pallas_call x0 -> x5, Pallas kernels: none -> 15.8 us  [the longest x1 7.48 us: local(): pl.pallas_call(main_kernel, out_shape=jax.ShapeDtypeStruct((32, 8, LANES)...]
    all_to_all x2 -> x0, starting transfers between devices: 11.1 us -> none  [sent_to_all(): return lax.all_to_all(copies, axis, split_axis=0, concat_axis=0, tiled=True)]
    dot_general x5 -> x0, matrix products: 9.72 us -> none  [the longest x1 3.65 us: local(): mixed = jnp.dot(whole_mix, message, preferred_element_type=jnp.float32)]
    ppermute x6 -> x4, starting transfers between devices: 21.8 us -> 12.7 us  [the longest x1 8.73 us: local(): pos_cross = lax.ppermute(positions, atoms, crossing)]
    gather x4 -> x0, local copies, waits for them, and re-layouts: 8.3 us -> none  [the longest x2 5.3 us: local(): far_feat = whole_feat[:, flat_index]]
  transfers between devices with their start and end apart: 9 -> 4, of which waited for: 4 -> 0; matrix products, arithmetic and copies ran while one was open for 7% -> 0% of each run, Pallas kernels for 0% -> 4%
where the time goes in v1:
time: 84.4 us; the launch traced here: 83.9 us
  blocking collectives  52 us (62%)
  Pallas kernels  15.8 us (19%)
  starting transfers between devices  12.7 us (15%)
  local copies, waits for them, and re-layouts  2.07 us (2%)
    all_to_all x1, blocking collectives, local(): gathered = lax.all_to_all(packed, ('y', 'zh'), 0, 0, tiled=True)  27.5 us
    all_to_all x1, blocking collectives, local(): got = lax.all_to_all(message, ('x', 'y', 'k'), 0, 0, tiled=True)  13.9 us
    all_to_all x1, blocking collectives, local(): got = lax.all_to_all(message, ('zl', 'zh'), 0, 0, tiled=True)  10.6 us
    ppermute x1, starting transfers between devices, local(): pos_cross = lax.ppermute(positions, atoms, crossing)  8.73 us
    pallas_call x1, Pallas kernels, local(): pl.pallas_call(main_kernel, out_shape=jax.ShapeDtypeStruct((32, 8, LANES)...  7.48 us
    pallas_call x1, Pallas kernels, local(): pl.pallas_call(stage_kernel, out_shape=(jax.ShapeDtypeStruct((channels, e...  3.43 us
    unnamed x12, local copies, waits for them, and re-layouts  2.04 us
    ppermute x1, starting transfers between devices, local(): swapped = lax.ppermute(gathered, atoms, siblings)  1.93 us
  transfers between devices with their start and end apart: 4, of which 0 were waited for; matrix products, arithmetic and copies ran while one was open for 0% of the time, Pallas kernels for 4%

profile of v1, /device:TPU:1, one launch (start us, length us, event | category | flops | bytes accessed | tf_op | source)
XLA Modules:
  0.0 83.9 jit_solution(13653445275697592074)
XLA Ops:
  0.6 0.6 pad_add_fusion.place
  1.3 1.8 %pack.1 = bf16[8,64,640]{2,1,0:T(8,128)(2,1)} custom-call(s32[4]{0:T(128)} %pad_add_fusion.place, bf16[64,128]{1,0:T(8,128)(2,1)} %feat.1, bf16[64,512]{1,0:T(8,128)(2,1)} %rout.1, bf16[64,512]{1,0:T(8,128)(2,1)} %bitcast.7), custom_call_target="tpu_custom_call" | custom-call | tf_op jit(solution)/shard_map/pack/pallas_call | solution.py:285
  3.1 0.0 copy-start.3
  3.1 27.5 %all_to_all.15.gathered = bf16[8,64,640]{2,1,0:T(8,128)(2,1)S(1)} all-to-all(bf16[8,64,640]{2,1,0:T(8,128)(2,1)} %pack.1), channel_id=1, replica_groups=mesh['x'=4,'zl'=4,'k'=2,'y'=4,'zh'=2] {'y','zh'}, dimensions={0} | all-to-all | bytes 1310720 | tf_op jit(solution)/shard_map/all_to_all | solution.py:292
  30.6 0.0 copy-start
  30.6 1.9 %collective-permute-start = (bf16[8,64,640]{2,1,0:T(8,128)(2,1)S(1)}, bf16[8,64,640]{2,1,0:T(8,128)(2,1)S(1)}, u32[]{:S(2)}, u32[]{:S(2)}) collective-permute-start(bf16[8,64,640]{2,1,0:T(8,128)(2,1)S(1)} %all_to_all.15.gathered), channel_id=1, source_target_pairs={{0,8},{8,0},{16,24},{24,16},{32,40},{40,32},{48,56},{56,48},{64,72... | collective-permute-start | bytes 1966088 | tf_op jit(solution)/shard_map/ppermute | solution.py:308
  32.5 0.0 copy-done.3
  32.5 0.1 collective-permute-start.2
  32.6 8.7 %collective-permute-start.3 = (f32[3,128]{1,0:T(4,128)S(1)}, f32[3,128]{1,0:T(4,128)S(1)}, u32[]{:S(2)}, u32[]{:S(2)}) collective-permute-start(f32[3,128]{1,0:T(4,128)S(1)} %copy-done.3), channel_id=1, source_target_pairs={{8,16},{24,32},{40,48},{56,64},{72,80},{88,96},{104,112},{120,128}... | collective-permute-start | bytes 4616 | tf_op jit(solution)/shard_map/ppermute | solution.py:294
  41.4 1.9 %collective-permute-start.1 = (bf16[8,64,128]{2,1,0:T(8,128)(2,1)S(1)}, bf16[8,64,128]{2,1,0:T(8,128)(2,1)S(1)}, u32[]{:S(2)}, u32[]{:S(2)}) collective-permute-start(bf16[8,64,128]{2,1,0:T(8,128)(2,1)S(1)} %slice.4), channel_id=1, source_target_pairs={{8,16},{24,32},{40,48},{56,64},{72,80},{88,96},{104,112},{120,128}... | collective-permute-start | bytes 393224 | tf_op jit(solution)/shard_map/ppermute | solution.py:309
  43.3 0.0 collective-permute-done.2.sib
  43.3 0.0 copy-start.4
  43.3 0.0 collective-permute-done.3.cross
  43.3 0.6 copy-done.4
  43.9 0.0 copy-start.5
  43.9 0.6 copy-done.5
  44.5 3.4 %stage.1 = (bf16[512,1024]{1,0:T(8,128)(2,1)}, bf16[512,1024]{1,0:T(8,128)(2,1)}, f32[4,8,128]{2,1,0:T(8,128)}) custom-call(s32[4]{0:T(128)} %pad_add_fusion.place, f32[3,128]{1,0:T(4,128)} %pos.1, f32[3,128]{1,0:T(4,128)} %copy-done.4, f32[3,128]{1,0:T(4,128)} %copy-done.5, s32[64,128]{1,0:T(8,128)} %slots.3, bf16[512,128]{1,0:T(8,128)(2,1)} %radial_in.1), custom_call_target="tpu_custom_call" | custom-call | flops 5000000000 | bytes 4000000 | tf_op jit(solution)/shard_map/stage/pallas_call | solution.py:296
  47.9 0.0 copy-done
  47.9 0.0 collective-permute-done.1.cross
  47.9 0.0 copy-start.2
  47.9 0.0 collective-permute-done.swapped
  47.9 0.0 copy-start.1
  47.9 0.6 copy-done.2
  48.6 0.3 copy-done.1
  48.8 7.5 %main.1 = f32[32,8,128]{2,1,0:T(8,128)} custom-call(s32[4]{0:T(128)} %pad_add_fusion.place, bf16[8,64,640]{2,1,0:T(8,128)(2,1)} %copy-done, bf16[8,64,640]{2,1,0:T(8,128)(2,1)} %copy-done.1, bf16[8,64,128]{2,1,0:T(8,128)(2,1)} %copy-done.2, bf16[512,1024]{1,0:T(8,128)(2,1)} %get-tuple-element.5.hidden, bf16[512,1024]{1,0:T(8,128)(2,1)} %get-tuple-element.6.dhidden, ...), custom_call_target="tpu_custom_call" | custom-call | tf_op jit(solution)/shard_map/main/pallas_call | solution.py:310
  56.3 13.9 %all_to_all.16.got = f32[32,8,128]{2,1,0:T(8,128)} all-to-all(f32[32,8,128]{2,1,0:T(8,128)} %main.1), channel_id=1, replica_groups=mesh['x'=4,'zl'=4,'k'=2,'y'=4,'zh'=2] {'x','y','k'}, dimensions={0} | all-to-all | bytes 262144 | tf_op jit(solution)/shard_map/all_to_all | solution.py:336
  70.2 1.6 %middle.1 = f32[8,8,128]{2,1,0:T(8,128)} custom-call(s32[4]{0:T(128)} %pad_add_fusion.place, f32[32,8,128]{2,1,0:T(8,128)} %all_to_all.16.got), custom_call_target="tpu_custom_call" | custom-call | tf_op jit(solution)/shard_map/middle/pallas_call | solution.py:337
  71.8 10.6 %all_to_all.17.got = f32[8,8,128]{2,1,0:T(8,128)} all-to-all(f32[8,8,128]{2,1,0:T(8,128)} %middle.1), channel_id=1, replica_groups=mesh['x'=4,'zl'=4,'k'=2,'y'=4,'zh'=2] {'zl','zh'}, dimensions={0} | all-to-all | bytes 65536 | tf_op jit(solution)/shard_map/all_to_all | solution.py:344
  82.4 1.5 %final.1 = (f32[3,128]{1,0:T(4,128)}, f32[9,32]{1,0:T(8,128)}) custom-call(s32[4]{0:T(128)} %pad_add_fusion.place, f32[8,8,128]{2,1,0:T(8,128)} %all_to_all.17.got), custom_call_target="tpu_custom_call" | custom-call | tf_op jit(solution)/shard_map/final/pallas_call | solution.py:345
  (1 shorter events, 0.0 us)
Async XLA Ops:
  3.1 29.5 %copy-start.3 = (f32[3,128]{1,0:T(4,128)S(1)}, f32[3,128]{1,0:T(4,128)}, u32[]{:S(2)}) copy-start(f32[3,128]{1,0:T(4,128)} %pos.1) | copy-start | bytes 4612
  30.6 17.3 %copy-start = (bf16[8,64,640]{2,1,0:T(8,128)(2,1)}, bf16[8,64,640]{2,1,0:T(8,128)(2,1)S(1)}, u32[]{:S(2)}) copy-start(bf16[8,64,640]{2,1,0:T(8,128)(2,1)S(1)} %all_to_all.15.gathered) | copy-start | bytes 1966084
  30.6 17.3 %collective-permute-start = (bf16[8,64,640]{2,1,0:T(8,128)(2,1)S(1)}, bf16[8,64,640]{2,1,0:T(8,128)(2,1)S(1)}, u32[]{:S(2)}, u32[]{:S(2)}) collective-permute-start(bf16[8,64,640]{2,1,0:T(8,128)(2,1)S(1)} %all_to_all.15.gathered), channel_id=1, source_target_pairs={{0,8},{8,0},{16,24},{24,16},{32,40},{40,32},{48,56},{56,48},{64,72... | collective-permute-start | bytes 1966088 | tf_op jit(solution)/shard_map/ppermute | solution.py:308
  32.5 10.8 %collective-permute-start.2 = (f32[3,128]{1,0:T(4,128)S(1)}, f32[3,128]{1,0:T(4,128)S(1)}, u32[]{:S(2)}, u32[]{:S(2)}) collective-permute-start(f32[3,128]{1,0:T(4,128)S(1)} %copy-done.3), channel_id=1, source_target_pairs={{0,8},{8,0},{16,24},{24,16},{32,40},{40,32},{48,56},{56,48},{64,72... | collective-permute-start | bytes 4616 | tf_op jit(solution)/shard_map/ppermute | solution.py:293
  32.6 10.7 %collective-permute-start.3 = (f32[3,128]{1,0:T(4,128)S(1)}, f32[3,128]{1,0:T(4,128)S(1)}, u32[]{:S(2)}, u32[]{:S(2)}) collective-permute-start(f32[3,128]{1,0:T(4,128)S(1)} %copy-done.3), channel_id=1, source_target_pairs={{8,16},{24,32},{40,48},{56,64},{72,80},{88,96},{104,112},{120,128}... | collective-permute-start | bytes 4616 | tf_op jit(solution)/shard_map/ppermute | solution.py:294
  41.4 6.5 %collective-permute-start.1 = (bf16[8,64,128]{2,1,0:T(8,128)(2,1)S(1)}, bf16[8,64,128]{2,1,0:T(8,128)(2,1)S(1)}, u32[]{:S(2)}, u32[]{:S(2)}) collective-permute-start(bf16[8,64,128]{2,1,0:T(8,128)(2,1)S(1)} %slice.4), channel_id=1, source_target_pairs={{8,16},{24,32},{40,48},{56,64},{72,80},{88,96},{104,112},{120,128}... | collective-permute-start | bytes 393224 | tf_op jit(solution)/shard_map/ppermute | solution.py:309
  43.3 0.6 copy-start.4
  43.9 0.6 copy-start.5
  47.9 0.7 copy-start.2
  47.9 0.9 %copy-start.1 = (bf16[8,64,640]{2,1,0:T(8,128)(2,1)}, bf16[8,64,640]{2,1,0:T(8,128)(2,1)S(1)}, u32[]{:S(2)}) copy-start(bf16[8,64,640]{2,1,0:T(8,128)(2,1)S(1)} %collective-permute-done.swapped) | copy-start | bytes 1966084

commit v2 on v1

v2 whole, which is shorter than its diff:
```python
import jax
import jax.numpy as jnp
from jax import lax
from jax.experimental import pallas as pl
from jax.experimental.pallas import tpu as pltpu
from jax.sharding import Mesh
from jax.sharding import PartitionSpec as P


RIM = 48
LANES = 128
CHUNK = 256
SHARPNESS = 40.0
REACH = 10.0
STRUCTS = 32

VMEM = pl.BlockSpec(memory_space=pltpu.VMEM)
F32 = jnp.float32
BF16 = jnp.bfloat16


def kernel(body, outs, mib, scratch=(), cost=1, space=pltpu.VMEM):
    def call(*args):
        return pl.pallas_call(
            body,
            out_shape=[jax.ShapeDtypeStruct(shape, dtype) for shape, dtype in outs],
            in_specs=[pl.BlockSpec(memory_space=space)] * len(args),
            out_specs=[VMEM] * len(outs),
            scratch_shapes=list(scratch),
            compiler_params=pltpu.CompilerParams(vmem_limit_bytes=mib << 20),
            cost_estimate=pl.CostEstimate(flops=cost * 1_000_000_000, bytes_accessed=100_000, transcendentals=0),
        )(*args)

    return call


def iota(shape, dim):
    return lax.broadcasted_iota(jnp.int32, shape, dim)


def dot(a, b):
    return jnp.dot(a, b, preferred_element_type=F32)


def dot_t(a, b):
    return lax.dot_general(a, b, (((1,), (1,)), ((), ())), preferred_element_type=F32)


def sigmoid(v):
    return 0.5 + 0.5 * jnp.tanh(0.5 * v)


def where_am_i():
    return lax.axis_index("x"), lax.axis_index("zl"), lax.axis_index("k")


def slot_group():
    return lax.axis_index("y") * 2 + lax.axis_index("zh")


def pack_kernel(feat, weights, feat_z, weights_z, out):
    rows = feat.shape[0]
    zh = lax.axis_index("zh")
    here, there = pl.multiple_of(zh * rows, rows), pl.multiple_of((1 - zh) * rows, rows)
    for c in range(out.shape[0]):
        out[c, pl.ds(here, rows), :LANES] = feat[...]
        out[c, pl.ds(here, rows), LANES:] = weights[...]
        out[c, pl.ds(there, rows), :LANES] = feat_z[...]
        out[c, pl.ds(there, rows), LANES:] = weights_z[...]


def halo_of(core, sib, cross, lane):
    low = jnp.where(core == 0, sib, cross)
    high = jnp.where(core == 0, cross, sib)
    return jnp.where(lane < 64, low, high)


def own_rows(ref):
    used = 8
    first = pl.multiple_of(slot_group() * used, used)
    return ref[pl.ds(first, used), :]


def slot_index(slots):
    rows = own_rows(slots)
    return (rows + iota(rows.shape, 1) - RIM) & 255


def stage_kernel(pos, sib, cross, slots, radial_in, hidden, dhidden, geo):
    core = lax.axis_index("k")
    idx = slot_index(slots)
    lane = iota(idx.shape, 1)
    inner = idx & 127
    vecs = []
    for p in range(3):
        own = jnp.broadcast_to(pos[p : p + 1, :], idx.shape)
        ring = halo_of(
            core,
            jnp.broadcast_to(sib[p : p + 1, :], idx.shape),
            jnp.broadcast_to(cross[p : p + 1, :], idx.shape),
            lane,
        )
        far = jnp.where(
            idx < 128,
            jnp.take_along_axis(own, inner, axis=1),
            jnp.take_along_axis(ring, inner, axis=1),
        )
        vecs.append(far - own)
    dist = jnp.sqrt(1.0 + (vecs[0] * vecs[0] + vecs[1] * vecs[1] + vecs[2] * vecs[2]))
    for p in range(3):
        geo[p] = vecs[p]
    geo[3] = dist
    count = radial_in.shape[1]
    centers = iota((count, LANES), 0).astype(F32) * (REACH / count)
    weights = radial_in[...]
    for k in range(8):
        offset = jnp.broadcast_to(dist[k : k + 1, :], (count, LANES)) - centers
        bump = jnp.exp(-SHARPNESS * offset * offset)
        slope = (-2.0 * SHARPNESS * offset * bump).astype(BF16)
        both = jnp.concatenate([bump.astype(BF16), slope], axis=1)
        pre2 = dot(weights, both)
        pre, dpre = pre2[:, :LANES], pre2[:, LANES:]
        sig = sigmoid(pre)
        silu = pre * sig
        at = slice(k * LANES, (k + 1) * LANES)
        hidden[:, at] = silu.astype(BF16)
        dhidden[:, at] = ((sig + silu * (1.0 - sig)) * dpre).astype(BF16)


def radial_kernel(gathered, swapped, hidden, dhidden, radial, dradial, mix, mixt):
    core = lax.axis_index("k")
    channels = mix.shape[0]

    def run(w_rad, w_mixt):
        weights = w_rad[:, :, LANES:].reshape(channels, channels)
        for n in range(hidden.shape[1] // CHUNK):
            at = slice(n * CHUNK, (n + 1) * CHUNK)
            radial[:, at] = dot(weights, hidden[:, at])
            dradial[:, at] = dot(weights, dhidden[:, at])
        turned = w_mixt[:, :, LANES:].reshape(channels, channels)
        mixt[...] = turned
        mix[...] = turned.T

    @pl.when(core == 0)
    def _():
        run(gathered, swapped)

    @pl.when(core != 0)
    def _():
        run(swapped, gathered)


def main_kernel(
    own, sib, cross, radial, dradial, mix, mixt, geo, slots, valid, ids, readout, out, table_f, scale
):
    core = lax.axis_index("k")
    channels = table_f.shape[0]
    lane = iota((channels, LANES), 1)
    own_f = own[:, :, :LANES].reshape(channels, LANES)
    sib_f = sib[:, :, :LANES].reshape(channels, LANES)
    cross_f = cross[...].reshape(channels, LANES)
    table_f[:, :LANES] = own_f
    table_f[:, LANES:] = halo_of(core, sib_f, cross_f, lane)
    turned = jnp.concatenate([readout[...]] * 2, axis=0).T
    for j in range(4):
        scale[j * LANES : (j + 1) * LANES, :] = jnp.broadcast_to(turned[:, j : j + 1], (LANES, LANES))

    idx = slot_index(slots)
    weight = own_rows(valid).astype(F32)
    gdists = []
    onehots = []
    for n in range(1024 // CHUNK):
        per = CHUNK // LANES
        row_of = iota((256, LANES), 0)
        onehot = jnp.concatenate(
            [
                (row_of == jnp.broadcast_to(idx[k : k + 1, :], (256, LANES))).astype(F32).astype(BF16)
                for k in range(n * per, (n + 1) * per)
            ],
            axis=1,
        )
        onehots.append(onehot)
        at = slice(n * CHUNK, (n + 1) * CHUNK)
        far = dot(table_f[...], onehot)
        message = (far * radial[:, at]).astype(BF16)
        mixed = dot(mix[...], message)
        sig = sigmoid(mixed)
        slope = sig + mixed * sig * (1.0 - sig)
        wide = jnp.concatenate([scale[...]] * per, axis=1)
        gmix = (wide * slope).astype(BF16)
        gmsg = dot(mixt[...], gmix)
        gdists.append(jnp.sum(gmsg * far * dradial[:, at], axis=0, keepdims=True))
    row8 = iota((8, LANES), 0)
    gdist = jnp.zeros((8, LANES), F32)
    for k in range(8):
        per = CHUNK // LANES
        part = gdists[k // per][:, (k % per) * LANES : (k % per + 1) * LANES]
        gdist = jnp.where(row8 == k, jnp.broadcast_to(part, (8, LANES)), gdist)
    over = gdist * weight / geo[3]
    vecs = [geo[p] for p in range(3)]
    gvec = [over * v for v in vecs]

    def total(v):
        return jnp.broadcast_to(jnp.sum(v, axis=0, keepdims=True), (8, LANES))

    zero = jnp.zeros((8, LANES), F32)
    acc = jnp.zeros((8, 256), F32)
    for k in range(8):
        rows = zero
        for p in range(3):
            rows = jnp.where(row8 == p, jnp.broadcast_to(gvec[p][k : k + 1, :], (8, LANES)), rows)
        per = CHUNK // LANES
        hot = onehots[k // per][:, (k % per) * LANES : (k % per + 1) * LANES]
        rest = rows
        for _ in range(3):
            part = rest.astype(BF16)
            acc = acc + dot_t(part, hot)
            rest = rest - part.astype(F32)
    mine, ring = -acc[:, :LANES], -acc[:, LANES:]
    for p in range(3):
        mine = mine + jnp.where(row8 == p, total(gvec[p]), 0.0)
    pairs = ((0, 0), (0, 1), (0, 2), (1, 1), (1, 2), (2, 2))
    vir = jnp.where(row8 == 6, 1.0, zero)
    for j, (p, q) in enumerate(pairs):
        vir = jnp.where(row8 == j, total(vecs[p] * gvec[q]), vir)
    struct = iota((LANES, LANES), 0) & (STRUCTS - 1)
    member = (struct == jnp.broadcast_to(ids[...], (LANES, LANES))).astype(F32).astype(BF16)
    spread = jnp.zeros((8, LANES), F32)
    rest = vir
    for _ in range(3):
        part = rest.astype(BF16)
        spread = spread + dot_t(part, member)
        rest = rest - part.astype(F32)
    lane8 = iota((8, LANES), 1)
    picked = jnp.where((lane8 >> 5) == (row8 & 3), spread, 0.0)
    first_row = total(jnp.where(row8 < 4, picked, 0.0))
    second_row = total(jnp.where(row8 >= 4, picked, 0.0))
    ring = pltpu.roll(ring, 3, 0)
    result = jnp.where(row8 < 3, mine, jnp.where(row8 < 6, ring, jnp.where(row8 == 6, first_row, second_row)))
    for c in range(out.shape[0]):
        out[c] = result


def middle_kernel(got, out):
    (x, zl, core), nx = where_am_i(), 4
    row8, lane8 = iota((8, LANES), 0), iota((8, LANES), 1)
    edge = jnp.where(core == 0, jnp.where(zl == 3, -1, 0), jnp.where(zl == 0, 1, 0))
    source = x + edge
    inside = jnp.logical_and(source >= 0, source < nx)
    source = jnp.clip(source, 0, nx - 1)
    whole = got[0]
    for i in range(1, got.shape[0]):
        whole = whole + got[i]

    def over_y(xx, kk):
        v = got[xx * 8 + kk]
        for y in range(1, 4):
            v = v + got[xx * 8 + y * 2 + kk]
        return v

    mine = over_y(x, core)
    near = pltpu.roll(over_y(x, 1 - core), 5, 0)
    far = over_y(source, 1 - core)
    far = jnp.where(inside, far, 0.0)
    low = lane8 < 64
    is_first = core == 0
    near_mask = jnp.logical_xor(low, is_first)
    mine = mine + jnp.where(near_mask, near, 0.0)
    far = jnp.where(near_mask, 0.0, far)
    result = jnp.where(row8 < 3, mine, jnp.where(row8 < 6, far, whole))
    for c in range(out.shape[0]):
        out[c] = result


def final_kernel(got, forces, stress):
    _, zl, core = where_am_i()
    whole = got[0]
    for i in range(1, got.shape[0]):
        whole = whole + got[i]
    mine = got[zl * 2] + got[zl * 2 + 1]
    other = (zl + jnp.where(core == 0, 3, 1)) & 3
    ring = got[other * 2] + got[other * 2 + 1]
    forces[...] = mine[:3, :] + ring[3:6, :]
    count = whole[7:8, 64:96] * 0.125
    where_is = {(0, 0): 0, (0, 1): 1, (0, 2): 2, (1, 1): 3, (1, 2): 4, (2, 2): 5}
    for p in range(3):
        for q in range(3):
            j = where_is[(min(p, q), max(p, q))]
            value = whole[6 + j // 4 : 7 + j // 4, (j % 4) * 32 : (j % 4) * 32 + 32]
            stress[3 * p + q : 3 * p + q + 1, :] = -value / count


def chip_to_chip():
    pairs = []
    for x in range(4):
        for zl in range(4):
            if x == 3 and zl == 3:
                continue
            for y in range(4):
                for zh in range(2):
                    here = (((x * 4 + zl) * 2 + 1) * 4 + y) * 2 + zh
                    if zl < 3:
                        there = (((x * 4 + zl + 1) * 2) * 4 + y) * 2 + zh
                    else:
                        there = ((((x + 1) * 4) * 2) * 4 + y) * 2 + (1 - zh)
                    pairs += [(here, there), (there, here)]
    return pairs


def z_partners(mirrored):
    pairs = []
    for x in range(4):
        for zl in range(4):
            for core in range(2):
                for y in range(4):
                    for zh in range(2):
                        other = 3 - zl if mirrored else zl
                        here = (((x * 4 + zl) * 2 + core) * 4 + y) * 2 + zh
                        there = (((x * 4 + other) * 2 + core) * 4 + y) * 2 + (1 - zh)
                        pairs.append((here, there))
    return pairs


def local(positions, features, struct_ids, slots, validity, radial_in, radial_out, mixing, readout):
    atoms = ("x", "zl", "k")
    domains = lax.axis_size(atoms)
    siblings = [(d, d ^ 1) for d in range(domains)]
    crossing = chip_to_chip()
    everyone = ("x", "zl", "k", "y", "zh")
    channels, edges = readout.shape[0], 8 * LANES
    rows = features.shape[0]
    feat_z = lax.ppermute(features, everyone, z_partners(False))
    weights = jnp.where(lax.axis_index("k") == 0, radial_out, mixing.T)
    weights_z = lax.ppermute(weights, everyone, z_partners(True))
    packed = kernel(pack_kernel, [((4, 2 * rows, LANES + channels), BF16)], 4)(
        features, weights, feat_z, weights_z
    )[0]
    gathered = lax.all_to_all(packed, "y", 0, 0, tiled=True)
    pos_sib = lax.ppermute(positions, atoms, siblings)
    pos_cross = lax.ppermute(positions, everyone, crossing)
    hidden, dhidden, geo = kernel(
        stage_kernel,
        [((channels, edges), BF16), ((channels, edges), BF16), ((4, 8, LANES), F32)],
        16,
        cost=3,
    )(positions, pos_sib, pos_cross, slots, radial_in)
    cross = lax.ppermute(gathered[:, :, :LANES], everyone, crossing)
    swapped = lax.ppermute(gathered, atoms, siblings)
    radial, dradial, mix, mixt = kernel(
        radial_kernel,
        [((channels, edges), F32)] * 2 + [((channels, channels), BF16)] * 2,
        12,
        cost=2,
    )(gathered, swapped, hidden, dhidden)
    message = kernel(
        main_kernel,
        [((32, 8, LANES), F32)],
        20,
        scratch=[pltpu.VMEM((channels, 2 * LANES), BF16), pltpu.VMEM((channels, LANES), F32)],
        cost=4,
    )(
        gathered,
        swapped,
        cross,
        radial,
        dradial,
        mix,
        mixt,
        geo,
        slots,
        validity,
        struct_ids.reshape(1, LANES),
        readout.reshape(4, LANES),
    )[0]
    got = lax.all_to_all(message, ("x", "y", "k"), 0, 0, tiled=True)
    message = kernel(middle_kernel, [((8, 8, LANES), F32)], 4)(got)[0]
    got = lax.all_to_all(message, ("zl", "zh"), 0, 0, tiled=True)
    return tuple(kernel(final_kernel, [((3, LANES), F32), ((9, STRUCTS), F32)], 4)(got))


def solution(mesh):
    fine = Mesh(mesh.devices.reshape(4, 4, 2, 4, 2), ("x", "zl", "k", "y", "zh"))
    atoms, chans = ("x", "zl", "k"), ("y", "zh")
    placed = (
        P(None, atoms),
        P(chans, atoms),
        P(atoms),
        P(None, atoms),
        P(None, atoms),
        P(),
        P(chans, None),
        P(None, chans),
        P(),
    )
    return jax.shard_map(
        local, mesh=fine, in_specs=placed, out_specs=(P(None, atoms), P()), check_vma=False
    )
```

time: 84.4 us -> 75.4 us (0.89)
  blocking collectives: 52 us -> 38.7 us
  waiting for transfers between devices: 0.01 us -> 8.63 us
  Pallas kernels: 15.8 us -> 7.23 us
  starting transfers between devices: 12.7 us -> 18.1 us
  local copies, waits for them, and re-layouts: 2.07 us -> 0.78 us
    all_to_all x1, blocking collectives: 27.5 us -> 12.6 us  [local(): gathered = lax.all_to_all(packed, 'y', 0, 0, tiled=True)]
    ppermute x2 -> x4, waiting for transfers between devices: 0.01 us -> 8.62 us  [the longest x1 5.75 us: local(): feat_z = lax.ppermute(features, everyone, z_partners(False))]
    pallas_call x5 -> x6, Pallas kernels: 15.8 us -> 7.23 us  [call(): pl.pallas_call(body, out_shape=[jax.ShapeDtypeStruct(shape, dtype) for sh...]
    ppermute x2 -> x4, starting transfers between devices: 10.7 us -> 14.8 us  [the longest x1 6.48 us: local(): weights_z = lax.ppermute(weights, everyone, z_partners(True))]
    all_to_all x1, blocking collectives: 13.9 us -> 17.3 us  [local(): got = lax.all_to_all(message, ('x', 'y', 'k'), 0, 0, tiled=True)]
    all_to_all x1, blocking collectives: 10.6 us -> 8.93 us  [local(): got = lax.all_to_all(message, ('zl', 'zh'), 0, 0, tiled=True)]
    ppermute x1, starting transfers between devices: 1.93 us -> 3.27 us  [local(): swapped = lax.ppermute(gathered, atoms, siblings)]
    unnamed x12 -> x14, local copies, waits for them, and re-layouts: 2.04 us -> 0.75 us
  transfers between devices with their start and end apart: 4 -> 6, of which waited for: 0 -> 3; matrix products, arithmetic and copies ran while one was open for 0% -> 0% of each run, Pallas kernels for 4% -> 3%
where the time goes in v2:
time: 75.4 us; the launch traced here: 75.1 us
  blocking collectives  38.7 us (51%)
  starting transfers between devices  18.1 us (24%)
  waiting for transfers between devices  8.63 us (11%)
  Pallas kernels  7.23 us (10%)
  other arithmetic  0.86 us (1%)
  local copies, waits for them, and re-layouts  0.78 us (1%)
  between operations  0.76 us (1%)
    all_to_all x1, blocking collectives, local(): got = lax.all_to_all(message, ('x', 'y', 'k'), 0, 0, tiled=True)  17.3 us
    all_to_all x1, blocking collectives, local(): gathered = lax.all_to_all(packed, 'y', 0, 0, tiled=True)  12.6 us
    all_to_all x1, blocking collectives, local(): got = lax.all_to_all(message, ('zl', 'zh'), 0, 0, tiled=True)  8.93 us
    pallas_call x6, Pallas kernels, call(): pl.pallas_call(body, out_shape=[jax.ShapeDtypeStruct(shape, dtype) for sh...  7.23 us
    ppermute x1, starting transfers between devices, local(): weights_z = lax.ppermute(weights, everyone, z_partners(True))  6.48 us
    ppermute x1, waiting for transfers between devices, local(): feat_z = lax.ppermute(features, everyone, z_partners(False))  5.75 us
    ppermute x1, starting transfers between devices, local(): cross = lax.ppermute(gathered[:, :, :LANES], everyone, crossing)  3.47 us
    ppermute x1, starting transfers between devices, local(): pos_cross = lax.ppermute(positions, everyone, crossing)  3.46 us
  transfers between devices with their start and end apart: 6, of which 3 were waited for; matrix products, arithmetic and copies ran while one was open for 0% of the time, Pallas kernels for 3%

profile of v2, /device:TPU:1, one launch (start us, length us, event | category | flops | bytes accessed | tf_op | source)
XLA Modules:
  0.0 75.1 jit_solution(9644626023122492392)
XLA Ops:
  0.6 0.0 copy-start.4
  0.6 0.9 %bitcast_select_fusion.weights = bf16[64,512]{1,0:T(8,128)(2,1)S(1)} fusion(bf16[64,512]{1,0:T(8,128)(2,1)} %param.15, bf16[512,64]{0,1:T(8,128)(2,1)} %param.16, pred[]{:T(512)S(6)} %eq.3), kind=kLoop, calls=%fused_computation | loop fusion | flops 32768 | bytes 196609 | tf_op jit(solution)/shard_map/jit(_where)/select_n | solution.py:333
  1.5 0.0 copy-start
  1.5 0.0 copy-start.1
  1.5 6.5 %collective-permute-start.1 = (bf16[64,512]{1,0:T(8,128)(2,1)S(1)}, bf16[64,512]{1,0:T(8,128)(2,1)S(1)}, u32[]{:S(2)}, u32[]{:S(2)}) collective-permute-start(bf16[64,512]{1,0:T(8,128)(2,1)S(1)} %bitcast_select_fusion.weights), channel_id=1, source_target_pairs={{0,49},{1,48},{2,51},{3,50},{4,53},{5,52},{6,55},{7,54},{8,57},{9,... | collective-permute-start | bytes 196616 | tf_op jit(solution)/shard_map/ppermute | solution.py:334
  8.0 1.4 %collective-permute-start = (bf16[64,128]{1,0:T(8,128)(2,1)}, bf16[64,128]{1,0:T(8,128)(2,1)S(1)}, u32[]{:S(2)}, u32[]{:S(2)}) collective-permute-start(bf16[64,128]{1,0:T(8,128)(2,1)} %feat.1), channel_id=1, source_target_pairs={{0,1},{1,0},{2,3},{3,2},{4,5},{5,4},{6,7},{7,6},{8,9},{9,8},{10,11... | collective-permute-start | bytes 49160 | tf_op jit(solution)/shard_map/ppermute | solution.py:332
  9.4 5.7 %collective-permute-done.feat_z = bf16[64,128]{1,0:T(8,128)(2,1)S(1)} collective-permute-done((bf16[64,128]{1,0:T(8,128)(2,1)}, bf16[64,128]{1,0:T(8,128)(2,1)S(1)}, u32[]{:S(2)}, u32[]{:S(2)}) %collective-permute-start) | collective-permute-done | bytes 16416 | tf_op jit(solution)/shard_map/ppermute | solution.py:332
  15.2 0.0 collective-permute-done.1.weights_z
  15.2 0.0 copy-start.3
  15.2 0.7 copy-done.3
  15.9 0.1 shard_map.104
  16.0 12.6 %all_to_all.15.gathered.own = bf16[4,128,640]{2,1,0:T(8,128)(2,1)S(1)} all-to-all(bf16[4,128,640]{2,1,0:T(8,128)(2,1)S(1)} %shard_map.104), channel_id=1, replica_groups=mesh['x'=4,'zl'=4,'k'=2,'y'=4,'zh'=2] {'y'}, dimensions={0} | all-to-all | bytes 1310720 | tf_op jit(solution)/shard_map/all_to_all | solution.py:338
  28.5 3.3 %collective-permute-start.2 = (bf16[4,128,640]{2,1,0:T(8,128)(2,1)S(1)}, bf16[4,128,640]{2,1,0:T(8,128)(2,1)S(1)}, u32[]{:S(2)}, u32[]{:S(2)}) collective-permute-start(bf16[4,128,640]{2,1,0:T(8,128)(2,1)S(1)} %all_to_all.15.gathered.own), channel_id=1, source_target_pairs={{0,8},{8,0},{16,24},{24,16},{32,40},{40,32},{48,56},{56,48},{64,72... | collective-permute-start | bytes 1966088 | tf_op jit(solution)/shard_map/ppermute | solution.py:348
  31.8 0.0 copy-done.4
  31.8 0.0 collective-permute-start.4
  31.8 3.5 %collective-permute-start.5 = (f32[3,128]{1,0:T(4,128)S(1)}, f32[3,128]{1,0:T(4,128)S(1)}, u32[]{:S(2)}, u32[]{:S(2)}) collective-permute-start(f32[3,128]{1,0:T(4,128)S(1)} %copy-done.4), channel_id=1, source_target_pairs={{8,16},{16,8},{9,17},{17,9},{10,18},{18,10},{11,19},{19,11},{12,20... | collective-permute-start | bytes 4616 | tf_op jit(solution)/shard_map/ppermute | solution.py:340
  35.3 0.0 collective-permute-done.4.sib
  35.3 1.4 %collective-permute-done.5.cross = f32[3,128]{1,0:T(4,128)S(1)} collective-permute-done((f32[3,128]{1,0:T(4,128)S(1)}, f32[3,128]{1,0:T(4,128)S(1)}, u32[]{:S(2)}, u32[]{:S(2)}) %collective-permute-start.5) | collective-permute-done | bytes 1568 | tf_op jit(solution)/shard_map/ppermute | solution.py:340
  36.7 0.0 copy-done
  36.7 0.0 copy-done.1
  36.7 1.1 %shard_map.105 = (bf16[512,1024]{1,0:T(8,128)(2,1)S(1)}, bf16[512,1024]{1,0:T(8,128)(2,1)S(1)}, f32[4,8,128]{2,1,0:T(8,128)S(1)}) custom-call(f32[3,128]{1,0:T(4,128)S(1)} %copy-done.4, f32[3,128]{1,0:T(4,128)S(1)} %collective-permute-done.4.sib, f32[3,128]{1,0:T(4,128)S(1)} %collective-permute-done.5.cross, s32[64,128]{1,0:T(8,128)S(1)} %copy-done.1, ...), custom_call_target="tpu_custom_call" | custom-call | flops 3000000000 | bytes 100000 | tf_op jit(solution)/shard_map/pallas_call | solution.py:24
  37.9 3.5 %collective-permute-start.3 = (bf16[4,128,128]{2,1,0:T(8,128)(2,1)S(1)}, bf16[4,128,128]{2,1,0:T(8,128)(2,1)S(1)}, u32[]{:S(2)}, u32[]{:S(2)}) collective-permute-start(bf16[4,128,128]{2,1,0:T(8,128)(2,1)S(1)} %slice.4), channel_id=1, source_target_pairs={{8,16},{16,8},{9,17},{17,9},{10,18},{18,10},{11,19},{19,11},{12,20... | collective-permute-start | bytes 393224 | tf_op jit(solution)/shard_map/ppermute | solution.py:347
  41.4 0.0 collective-permute-done.2.swapped.sib
  41.4 0.0 copy-start.2
  41.4 0.0 copy-start.5
  41.4 0.0 copy-start.6
  41.4 1.3 %shard_map.106 = (f32[512,1024]{1,0:T(8,128)S(1)}, f32[512,1024]{1,0:T(8,128)S(1)}, bf16[512,512]{1,0:T(8,128)(2,1)S(1)}, bf16[512,512]{1,0:T(8,128)(2,1)S(1)}) custom-call(bf16[4,128,640]{2,1,0:T(8,128)(2,1)S(1)} %all_to_all.15.gathered.own, bf16[4,128,640]{2,1,0:T(8,128)(2,1)S(1)} %collective-permute-done.2.swapped.sib, ...), custom_call_target="tpu_custom_call" | custom-call | flops 2000000000 | bytes 100000 | tf_op jit(solution)/shard_map/pallas_call | solution.py:24
  42.7 1.5 %collective-permute-done.3.cross = bf16[4,128,128]{2,1,0:T(8,128)(2,1)S(1)} collective-permute-done((bf16[4,128,128]{2,1,0:T(8,128)(2,1)S(1)}, bf16[4,128,128]{2,1,0:T(8,128)(2,1)S(1)}, u32[]{:S(2)}, u32[]{:S(2)}) %collective-permute-start.3) | collective-permute-done | bytes 131104 | tf_op jit(solution)/shard_map/ppermute | solution.py:347
  44.2 0.0 copy-done.2
  44.2 0.0 copy-done.5
  44.2 0.0 copy-done.6
  44.2 3.9 %shard_map.107 = f32[32,8,128]{2,1,0:T(8,128)S(1)} custom-call(bf16[4,128,640]{2,1,0:T(8,128)(2,1)S(1)} %all_to_all.15.gathered.own, bf16[4,128,640]{2,1,0:T(8,128)(2,1)S(1)} %collective-permute-done.2.swapped.sib, bf16[4,128,128]{2,1,0:T(8,128)(2,1)S(1)} %collective-permute-done.3.cross, f32[512,1024]{1,0:T(8,128)S(1)} %get-tuple-element.11.radial, ...), custom_call_target="tpu_custom_call" | custom-call | flops 4000000000 | bytes 100000 | tf_op jit(solution)/shard_map/pallas_call | solution.py:24
  48.1 17.3 %all_to_all.16.got = f32[32,8,128]{2,1,0:T(8,128)S(1)} all-to-all(f32[32,8,128]{2,1,0:T(8,128)S(1)} %shard_map.107), channel_id=1, replica_groups=mesh['x'=4,'zl'=4,'k'=2,'y'=4,'zh'=2] {'x','y','k'}, dimensions={0} | all-to-all | bytes 262144 | tf_op jit(solution)/shard_map/all_to_all | solution.py:375
  65.4 8.9 %all_to_all.17.got = f32[8,8,128]{2,1,0:T(8,128)S(1)} all-to-all(f32[8,8,128]{2,1,0:T(8,128)S(1)} %shard_map.108), channel_id=1, replica_groups=mesh['x'=4,'zl'=4,'k'=2,'y'=4,'zh'=2] {'zl','zh'}, dimensions={0} | all-to-all | bytes 65536 | tf_op jit(solution)/shard_map/all_to_all | solution.py:377
  74.4 0.8 %shard_map.109 = (f32[3,128]{1,0:T(4,128)}, f32[9,32]{1,0:T(8,128)}) custom-call(f32[8,8,128]{2,1,0:T(8,128)S(1)} %all_to_all.17.got), custom_call_target="tpu_custom_call" | custom-call | flops 1000000000 | bytes 100000 | tf_op jit(solution)/shard_map/pallas_call | solution.py:24
  (2 shorter events, 0.1 us)
Async XLA Ops:
  0.6 31.2 %copy-start.4 = (f32[3,128]{1,0:T(4,128)S(1)}, f32[3,128]{1,0:T(4,128)}, u32[]{:S(2)}) copy-start(f32[3,128]{1,0:T(4,128)} %pos.1) | copy-start | bytes 4612
  1.5 35.2 %copy-start = (bf16[512,128]{1,0:T(8,128)(2,1)S(1)}, bf16[512,128]{1,0:T(8,128)(2,1)}, u32[]{:S(2)}) copy-start(bf16[512,128]{1,0:T(8,128)(2,1)} %radial_in.1) | copy-start | bytes 393220
  1.5 35.2 %copy-start.1 = (s32[64,128]{1,0:T(8,128)S(1)}, s32[64,128]{1,0:T(8,128)}, u32[]{:S(2)}) copy-start(s32[64,128]{1,0:T(8,128)} %slots.3) | copy-start | bytes 98308
  1.5 13.7 %collective-permute-start.1 = (bf16[64,512]{1,0:T(8,128)(2,1)S(1)}, bf16[64,512]{1,0:T(8,128)(2,1)S(1)}, u32[]{:S(2)}, u32[]{:S(2)}) collective-permute-start(bf16[64,512]{1,0:T(8,128)(2,1)S(1)} %bitcast_select_fusion.weights), channel_id=1, source_target_pairs={{0,49},{1,48},{2,51},{3,50},{4,53},{5,52},{6,55},{7,54},{8,57},{9,... | collective-permute-start | bytes 196616 | tf_op jit(solution)/shard_map/ppermute | solution.py:334
  8.0 7.2 %collective-permute-start = (bf16[64,128]{1,0:T(8,128)(2,1)}, bf16[64,128]{1,0:T(8,128)(2,1)S(1)}, u32[]{:S(2)}, u32[]{:S(2)}) collective-permute-start(bf16[64,128]{1,0:T(8,128)(2,1)} %feat.1), channel_id=1, source_target_pairs={{0,1},{1,0},{2,3},{3,2},{4,5},{5,4},{6,7},{7,6},{8,9},{9,8},{10,11... | collective-permute-start | bytes 49160 | tf_op jit(solution)/shard_map/ppermute | solution.py:332
  15.2 0.7 copy-start.3
  28.5 12.8 %collective-permute-start.2 = (bf16[4,128,640]{2,1,0:T(8,128)(2,1)S(1)}, bf16[4,128,640]{2,1,0:T(8,128)(2,1)S(1)}, u32[]{:S(2)}, u32[]{:S(2)}) collective-permute-start(bf16[4,128,640]{2,1,0:T(8,128)(2,1)S(1)} %all_to_all.15.gathered.own), channel_id=1, source_target_pairs={{0,8},{8,0},{16,24},{24,16},{32,40},{40,32},{48,56},{56,48},{64,72... | collective-permute-start | bytes 1966088 | tf_op jit(solution)/shard_map/ppermute | solution.py:348
  31.8 3.5 %collective-permute-start.4 = (f32[3,128]{1,0:T(4,128)S(1)}, f32[3,128]{1,0:T(4,128)S(1)}, u32[]{:S(2)}, u32[]{:S(2)}) collective-permute-start(f32[3,128]{1,0:T(4,128)S(1)} %copy-done.4), channel_id=1, source_target_pairs={{0,8},{8,0},{16,24},{24,16},{32,40},{40,32},{48,56},{56,48},{64,72... | collective-permute-start | bytes 4616 | tf_op jit(solution)/shard_map/ppermute | solution.py:339
  31.8 4.9 %collective-permute-start.5 = (f32[3,128]{1,0:T(4,128)S(1)}, f32[3,128]{1,0:T(4,128)S(1)}, u32[]{:S(2)}, u32[]{:S(2)}) collective-permute-start(f32[3,128]{1,0:T(4,128)S(1)} %copy-done.4), channel_id=1, source_target_pairs={{8,16},{16,8},{9,17},{17,9},{10,18},{18,10},{11,19},{19,11},{12,20... | collective-permute-start | bytes 4616 | tf_op jit(solution)/shard_map/ppermute | solution.py:340
  37.9 6.3 %collective-permute-start.3 = (bf16[4,128,128]{2,1,0:T(8,128)(2,1)S(1)}, bf16[4,128,128]{2,1,0:T(8,128)(2,1)S(1)}, u32[]{:S(2)}, u32[]{:S(2)}) collective-permute-start(bf16[4,128,128]{2,1,0:T(8,128)(2,1)S(1)} %slice.4), channel_id=1, source_target_pairs={{8,16},{16,8},{9,17},{17,9},{10,18},{18,10},{11,19},{19,11},{12,20... | collective-permute-start | bytes 393224 | tf_op jit(solution)/shard_map/ppermute | solution.py:347
  41.4 2.8 %copy-start.2 = (s32[64,128]{1,0:T(8,128)S(1)}, s32[64,128]{1,0:T(8,128)}, u32[]{:S(2)}) copy-start(s32[64,128]{1,0:T(8,128)} %valid.1) | copy-start | bytes 98308
  41.4 2.8 %copy-start.5 = (f32[512]{0:T(512)S(1)}, f32[512]{0:T(512)}, u32[]{:S(2)}) copy-start(f32[512]{0:T(512)} %param.17) | copy-start | bytes 6148
  41.4 2.8 %copy-start.6 = (s32[128]{0:T(128)S(1)}, s32[128]{0:T(128)}, u32[]{:S(2)}) copy-start(s32[128]{0:T(128)} %param.11) | copy-start | bytes 1540

commit v3 on v2

--- a/solution.py
+++ b/solution.py
@@ -58,15 +58,13 @@
     return lax.axis_index("y") * 2 + lax.axis_index("zh")
 
 
-def pack_kernel(feat, weights, feat_z, weights_z, out):
-    rows = feat.shape[0]
+def pack_kernel(here_shard, there_shard, out):
+    rows = here_shard.shape[0]
     zh = lax.axis_index("zh")
     here, there = pl.multiple_of(zh * rows, rows), pl.multiple_of((1 - zh) * rows, rows)
     for c in range(out.shape[0]):
-        out[c, pl.ds(here, rows), :LANES] = feat[...]
-        out[c, pl.ds(here, rows), LANES:] = weights[...]
-        out[c, pl.ds(there, rows), :LANES] = feat_z[...]
-        out[c, pl.ds(there, rows), LANES:] = weights_z[...]
+        out[c, pl.ds(here, rows), :] = here_shard[...]
+        out[c, pl.ds(there, rows), :] = there_shard[...]
 
 
 def halo_of(core, sib, cross, lane):
@@ -294,30 +292,12 @@
     pairs = []
     for x in range(4):
         for zl in range(4):
-            if x == 3 and zl == 3:
-                continue
             for y in range(4):
                 for zh in range(2):
                     here = (((x * 4 + zl) * 2 + 1) * 4 + y) * 2 + zh
-                    if zl < 3:
-                        there = (((x * 4 + zl + 1) * 2) * 4 + y) * 2 + zh
-                    else:
-                        there = ((((x + 1) * 4) * 2) * 4 + y) * 2 + (1 - zh)
+                    x2, zl2, zh2 = (x + (zl == 3)) % 4, (zl + 1) % 4, zh ^ (zl == 3)
+                    there = ((x2 * 4 + zl2) * 2 * 4 + y) * 2 + zh2
                     pairs += [(here, there), (there, here)]
-    return pairs
-
-
-def z_partners(mirrored):
-    pairs = []
-    for x in range(4):
-        for zl in range(4):
-            for core in range(2):
-                for y in range(4):
-                    for zh in range(2):
-                        other = 3 - zl if mirrored else zl
-                        here = (((x * 4 + zl) * 2 + core) * 4 + y) * 2 + zh
-                        there = (((x * 4 + other) * 2 + core) * 4 + y) * 2 + (1 - zh)
-                        pairs.append((here, there))
     return pairs
 
 
@@ -329,12 +309,10 @@
     everyone = ("x", "zl", "k", "y", "zh")
     channels, edges = readout.shape[0], 8 * LANES
     rows = features.shape[0]
-    feat_z = lax.ppermute(features, everyone, z_partners(False))
     weights = jnp.where(lax.axis_index("k") == 0, radial_out, mixing.T)
-    weights_z = lax.ppermute(weights, everyone, z_partners(True))
-    packed = kernel(pack_kernel, [((4, 2 * rows, LANES + channels), BF16)], 4)(
-        features, weights, feat_z, weights_z
-    )[0]
+    shard = jnp.concatenate([features, weights], axis=1)
+    shard_z = lax.ppermute(shard, "zh", [(0, 1), (1, 0)])
+    packed = kernel(pack_kernel, [((4, 2 * rows, LANES + channels), BF16)], 4)(shard, shard_z)[0]
     gathered = lax.all_to_all(packed, "y", 0, 0, tiled=True)
     pos_sib = lax.ppermute(positions, atoms, siblings)
     pos_cross = lax.ppermute(positions, everyone, crossing)
@@ -356,7 +334,10 @@
         main_kernel,
         [((32, 8, LANES), F32)],
         20,
-        scratch=[pltpu.VMEM((channels, 2 * LANES), BF16), pltpu.VMEM((channels, LANES), F32)],
+        scratch=[
+            pltpu.VMEM((channels, 2 * LANES), BF16),
+            pltpu.VMEM((channels, LANES), F32),
+        ],
         cost=4,
     )(
         gathered,

time: 75.4 us -> 73.4 us (0.973)
  blocking collectives: 38.7 us -> 44.4 us
  starting transfers between devices: 18.1 us -> 13.4 us
  waiting for transfers between devices: 8.63 us -> 5.74 us
    ppermute x2 -> x1, waiting for transfers between devices: 5.75 us -> 1.93 us  [local(): shard_z = lax.ppermute(shard, 'zh', [(0, 1), (1, 0)])]
    all_to_all x1, blocking collectives: 8.93 us -> 12 us  [local(): got = lax.all_to_all(message, ('zl', 'zh'), 0, 0, tiled=True)]
    all_to_all x1, blocking collectives: 17.3 us -> 19.7 us  [local(): got = lax.all_to_all(message, ('x', 'y', 'k'), 0, 0, tiled=True)]
    ppermute x1, starting transfers between devices: 3.46 us -> 1.14 us  [local(): pos_cross = lax.ppermute(positions, everyone, crossing)]
    ppermute x1, starting transfers between devices: 3.47 us -> 1.23 us  [local(): cross = lax.ppermute(gathered[:, :, :LANES], everyone, crossing)]
    ppermute x2 -> x1, starting transfers between devices: 7.91 us -> 7.81 us  [local(): shard_z = lax.ppermute(shard, 'zh', [(0, 1), (1, 0)])]
  transfers between devices with their start and end apart: 6 -> 5, of which waited for: 3 -> 4; matrix products, arithmetic and copies ran while one was open for 0% -> 0% of each run, Pallas kernels for 3% -> 3%
where the time goes in v3:
time: 73.4 us; the launch traced here: 73.1 us
  blocking collectives  44.4 us (60%)
  starting transfers between devices  13.4 us (18%)
  Pallas kernels  7.23 us (10%)
  waiting for transfers between devices  5.74 us (8%)
  other arithmetic  1.59 us (2%)
    all_to_all x1, blocking collectives, local(): got = lax.all_to_all(message, ('x', 'y', 'k'), 0, 0, tiled=True)  19.7 us
    all_to_all x1, blocking collectives, local(): gathered = lax.all_to_all(packed, 'y', 0, 0, tiled=True)  12.6 us
    all_to_all x1, blocking collectives, local(): got = lax.all_to_all(message, ('zl', 'zh'), 0, 0, tiled=True)  12 us
    ppermute x1, starting transfers between devices, local(): shard_z = lax.ppermute(shard, 'zh', [(0, 1), (1, 0)])  7.81 us
    pallas_call x6, Pallas kernels, call(): pl.pallas_call(body, out_shape=[jax.ShapeDtypeStruct(shape, dtype) for sh...  7.23 us
    ppermute x1, starting transfers between devices, local(): swapped = lax.ppermute(gathered, atoms, siblings)  3.21 us
    ppermute x1, waiting for transfers between devices, local(): shard_z = lax.ppermute(shard, 'zh', [(0, 1), (1, 0)])  1.93 us
    ppermute x1, waiting for transfers between devices, local(): cross = lax.ppermute(gathered[:, :, :LANES], everyone, crossing)  1.93 us
  transfers between devices with their start and end apart: 5, of which 4 were waited for; matrix products, arithmetic and copies ran while one was open for 0% of the time, Pallas kernels for 3%

profile of v3, /device:TPU:1, one launch (start us, length us, event | category | flops | bytes accessed | tf_op | source)
XLA Modules:
  0.0 73.1 jit_solution(3981642661306793777)
XLA Ops:
  0.6 0.9 %bitcast_select_fusion = bf16[64,512]{1,0:T(8,128)(2,1)S(1)} fusion(bf16[64,512]{1,0:T(8,128)(2,1)} %param.15, bf16[512,64]{0,1:T(8,128)(2,1)} %param.16, pred[]{:T(512)S(6)} %eq.3), kind=kLoop, calls=%fused_computation.1 | loop fusion | flops 32768 | bytes 196609 | tf_op jit(solution)/shard_map/jit(_where)/select_n | solution.py:312
  1.5 0.7 pad_maximum_fusion.here_shard
  2.2 0.0 copy-start.3
  2.2 0.0 copy-start
  2.3 0.0 copy-start.1
  2.3 7.8 %collective-permute-start = (bf16[64,640]{1,0:T(8,128)(2,1)S(1)}, bf16[64,640]{1,0:T(8,128)(2,1)S(1)}, u32[]{:S(2)}, u32[]{:S(2)}) collective-permute-start(bf16[64,640]{1,0:T(8,128)(2,1)S(1)} %pad_maximum_fusion.here_shard), channel_id=1, source_target_pairs={{0,1},{1,0},{2,3},{3,2},{4,5},{5,4},{6,7},{7,6},{8,9},{9,8},{10,11... | collective-permute-start | bytes 245768 | tf_op jit(solution)/shard_map/ppermute | solution.py:314
  10.1 1.9 %collective-permute-done.there_shard = bf16[64,640]{1,0:T(8,128)(2,1)S(1)} collective-permute-done((bf16[64,640]{1,0:T(8,128)(2,1)S(1)}, bf16[64,640]{1,0:T(8,128)(2,1)S(1)}, u32[]{:S(2)}, u32[]{:S(2)}) %collective-permute-start) | collective-permute-done | bytes 81952 | tf_op jit(solution)/shard_map/ppermute | solution.py:314
  12.0 0.1 shard_map.104
  12.1 12.6 %all_to_all.15.gathered.own = bf16[4,128,640]{2,1,0:T(8,128)(2,1)S(1)} all-to-all(bf16[4,128,640]{2,1,0:T(8,128)(2,1)S(1)} %shard_map.104), channel_id=1, replica_groups=mesh['x'=4,'zl'=4,'k'=2,'y'=4,'zh'=2] {'y'}, dimensions={0} | all-to-all | bytes 1310720 | tf_op jit(solution)/shard_map/all_to_all | solution.py:316
  24.7 3.2 %collective-permute-start.1 = (bf16[4,128,640]{2,1,0:T(8,128)(2,1)S(1)}, bf16[4,128,640]{2,1,0:T(8,128)(2,1)S(1)}, u32[]{:S(2)}, u32[]{:S(2)}) collective-permute-start(bf16[4,128,640]{2,1,0:T(8,128)(2,1)S(1)} %all_to_all.15.gathered.own), channel_id=1, source_target_pairs={{0,8},{8,0},{16,24},{24,16},{32,40},{40,32},{48,56},{56,48},{64,72... | collective-permute-start | bytes 1966088 | tf_op jit(solution)/shard_map/ppermute | solution.py:326
  27.9 0.0 copy-done.3
  27.9 0.0 collective-permute-start.3
  27.9 1.1 %collective-permute-start.4 = (f32[3,128]{1,0:T(4,128)S(1)}, f32[3,128]{1,0:T(4,128)S(1)}, u32[]{:S(2)}, u32[]{:S(2)}) collective-permute-start(f32[3,128]{1,0:T(4,128)S(1)} %copy-done.3), channel_id=1, source_target_pairs={{8,16},{16,8},{9,17},{17,9},{10,18},{18,10},{11,19},{19,11},{12,20... | collective-permute-start | bytes 4616 | tf_op jit(solution)/shard_map/ppermute | solution.py:318
  29.0 0.6 collective-permute-done.3.sib
  29.6 1.3 %collective-permute-done.4.cross = f32[3,128]{1,0:T(4,128)S(1)} collective-permute-done((f32[3,128]{1,0:T(4,128)S(1)}, f32[3,128]{1,0:T(4,128)S(1)}, u32[]{:S(2)}, u32[]{:S(2)}) %collective-permute-start.4) | collective-permute-done | bytes 1568 | tf_op jit(solution)/shard_map/ppermute | solution.py:318
  30.9 0.0 copy-done
  30.9 0.0 copy-done.1
  30.9 1.1 %shard_map.105 = (bf16[512,1024]{1,0:T(8,128)(2,1)S(1)}, bf16[512,1024]{1,0:T(8,128)(2,1)S(1)}, f32[4,8,128]{2,1,0:T(8,128)S(1)}) custom-call(f32[3,128]{1,0:T(4,128)S(1)} %copy-done.3, f32[3,128]{1,0:T(4,128)S(1)} %collective-permute-done.3.sib, f32[3,128]{1,0:T(4,128)S(1)} %collective-permute-done.4.cross, s32[64,128]{1,0:T(8,128)S(1)} %copy-done.1, ...), custom_call_target="tpu_custom_call" | custom-call | flops 3000000000 | bytes 100000 | tf_op jit(solution)/shard_map/pallas_call | solution.py:24
  32.1 1.2 %collective-permute-start.2 = (bf16[4,128,128]{2,1,0:T(8,128)(2,1)S(1)}, bf16[4,128,128]{2,1,0:T(8,128)(2,1)S(1)}, u32[]{:S(2)}, u32[]{:S(2)}) collective-permute-start(bf16[4,128,128]{2,1,0:T(8,128)(2,1)S(1)} %slice.4), channel_id=1, source_target_pairs={{8,16},{16,8},{9,17},{17,9},{10,18},{18,10},{11,19},{19,11},{12,20... | collective-permute-start | bytes 393224 | tf_op jit(solution)/shard_map/ppermute | solution.py:325
  33.3 0.0 collective-permute-done.1.swapped.sib
  33.3 0.0 copy-start.2
  33.3 0.0 copy-start.4
  33.3 0.0 copy-start.5
  33.3 1.3 %shard_map.106 = (f32[512,1024]{1,0:T(8,128)S(1)}, f32[512,1024]{1,0:T(8,128)S(1)}, bf16[512,512]{1,0:T(8,128)(2,1)S(1)}, bf16[512,512]{1,0:T(8,128)(2,1)S(1)}) custom-call(bf16[4,128,640]{2,1,0:T(8,128)(2,1)S(1)} %all_to_all.15.gathered.own, bf16[4,128,640]{2,1,0:T(8,128)(2,1)S(1)} %collective-permute-done.1.swapped.sib, ...), custom_call_target="tpu_custom_call" | custom-call | flops 2000000000 | bytes 100000 | tf_op jit(solution)/shard_map/pallas_call | solution.py:24
  34.6 1.9 %collective-permute-done.2.cross = bf16[4,128,128]{2,1,0:T(8,128)(2,1)S(1)} collective-permute-done((bf16[4,128,128]{2,1,0:T(8,128)(2,1)S(1)}, bf16[4,128,128]{2,1,0:T(8,128)(2,1)S(1)}, u32[]{:S(2)}, u32[]{:S(2)}) %collective-permute-start.2) | collective-permute-done | bytes 131104 | tf_op jit(solution)/shard_map/ppermute | solution.py:325
  36.6 0.0 copy-done.2
  36.6 0.0 copy-done.4
  36.6 0.0 copy-done.5
  36.6 3.9 %shard_map.107 = f32[32,8,128]{2,1,0:T(8,128)S(1)} custom-call(bf16[4,128,640]{2,1,0:T(8,128)(2,1)S(1)} %all_to_all.15.gathered.own, bf16[4,128,640]{2,1,0:T(8,128)(2,1)S(1)} %collective-permute-done.1.swapped.sib, bf16[4,128,128]{2,1,0:T(8,128)(2,1)S(1)} %collective-permute-done.2.cross, f32[512,1024]{1,0:T(8,128)S(1)} %get-tuple-element.11.radial, ...), custom_call_target="tpu_custom_call" | custom-call | flops 4000000000 | bytes 100000 | tf_op jit(solution)/shard_map/pallas_call | solution.py:24
  40.5 19.7 %all_to_all.16.got = f32[32,8,128]{2,1,0:T(8,128)S(1)} all-to-all(f32[32,8,128]{2,1,0:T(8,128)S(1)} %shard_map.107), channel_id=1, replica_groups=mesh['x'=4,'zl'=4,'k'=2,'y'=4,'zh'=2] {'x','y','k'}, dimensions={0} | all-to-all | bytes 262144 | tf_op jit(solution)/shard_map/all_to_all | solution.py:356
  60.3 12.0 %all_to_all.17.got = f32[8,8,128]{2,1,0:T(8,128)S(1)} all-to-all(f32[8,8,128]{2,1,0:T(8,128)S(1)} %shard_map.108), channel_id=1, replica_groups=mesh['x'=4,'zl'=4,'k'=2,'y'=4,'zh'=2] {'zl','zh'}, dimensions={0} | all-to-all | bytes 65536 | tf_op jit(solution)/shard_map/all_to_all | solution.py:358
  72.3 0.8 %shard_map.109 = (f32[3,128]{1,0:T(4,128)}, f32[9,32]{1,0:T(8,128)}) custom-call(f32[8,8,128]{2,1,0:T(8,128)S(1)} %all_to_all.17.got), custom_call_target="tpu_custom_call" | custom-call | flops 1000000000 | bytes 100000 | tf_op jit(solution)/shard_map/pallas_call | solution.py:24
  (2 shorter events, 0.1 us)
Async XLA Ops:
  2.2 25.7 %copy-start.3 = (f32[3,128]{1,0:T(4,128)S(1)}, f32[3,128]{1,0:T(4,128)}, u32[]{:S(2)}) copy-start(f32[3,128]{1,0:T(4,128)} %pos.1) | copy-start | bytes 4612
  2.2 28.7 %copy-start = (bf16[512,128]{1,0:T(8,128)(2,1)S(1)}, bf16[512,128]{1,0:T(8,128)(2,1)}, u32[]{:S(2)}) copy-start(bf16[512,128]{1,0:T(8,128)(2,1)} %radial_in.1) | copy-start | bytes 393220
  2.3 28.7 %copy-start.1 = (s32[64,128]{1,0:T(8,128)S(1)}, s32[64,128]{1,0:T(8,128)}, u32[]{:S(2)}) copy-start(s32[64,128]{1,0:T(8,128)} %slots.3) | copy-start | bytes 98308
  2.3 9.7 %collective-permute-start = (bf16[64,640]{1,0:T(8,128)(2,1)S(1)}, bf16[64,640]{1,0:T(8,128)(2,1)S(1)}, u32[]{:S(2)}, u32[]{:S(2)}) collective-permute-start(bf16[64,640]{1,0:T(8,128)(2,1)S(1)} %pad_maximum_fusion.here_shard), channel_id=1, source_target_pairs={{0,1},{1,0},{2,3},{3,2},{4,5},{5,4},{6,7},{7,6},{8,9},{9,8},{10,11... | collective-permute-start | bytes 245768 | tf_op jit(solution)/shard_map/ppermute | solution.py:314
  24.7 8.6 %collective-permute-start.1 = (bf16[4,128,640]{2,1,0:T(8,128)(2,1)S(1)}, bf16[4,128,640]{2,1,0:T(8,128)(2,1)S(1)}, u32[]{:S(2)}, u32[]{:S(2)}) collective-permute-start(bf16[4,128,640]{2,1,0:T(8,128)(2,1)S(1)} %all_to_all.15.gathered.own), channel_id=1, source_target_pairs={{0,8},{8,0},{16,24},{24,16},{32,40},{40,32},{48,56},{56,48},{64,72... | collective-permute-start | bytes 1966088 | tf_op jit(solution)/shard_map/ppermute | solution.py:326
  27.9 1.7 %collective-permute-start.3 = (f32[3,128]{1,0:T(4,128)S(1)}, f32[3,128]{1,0:T(4,128)S(1)}, u32[]{:S(2)}, u32[]{:S(2)}) collective-permute-start(f32[3,128]{1,0:T(4,128)S(1)} %copy-done.3), channel_id=1, source_target_pairs={{0,8},{8,0},{16,24},{24,16},{32,40},{40,32},{48,56},{56,48},{64,72... | collective-permute-start | bytes 4616 | tf_op jit(solution)/shard_map/ppermute | solution.py:317
  27.9 3.0 %collective-permute-start.4 = (f32[3,128]{1,0:T(4,128)S(1)}, f32[3,128]{1,0:T(4,128)S(1)}, u32[]{:S(2)}, u32[]{:S(2)}) collective-permute-start(f32[3,128]{1,0:T(4,128)S(1)} %copy-done.3), channel_id=1, source_target_pairs={{8,16},{16,8},{9,17},{17,9},{10,18},{18,10},{11,19},{19,11},{12,20... | collective-permute-start | bytes 4616 | tf_op jit(solution)/shard_map/ppermute | solution.py:318
  32.1 4.5 %collective-permute-start.2 = (bf16[4,128,128]{2,1,0:T(8,128)(2,1)S(1)}, bf16[4,128,128]{2,1,0:T(8,128)(2,1)S(1)}, u32[]{:S(2)}, u32[]{:S(2)}) collective-permute-start(bf16[4,128,128]{2,1,0:T(8,128)(2,1)S(1)} %slice.4), channel_id=1, source_target_pairs={{8,16},{16,8},{9,17},{17,9},{10,18},{18,10},{11,19},{19,11},{12,20... | collective-permute-start | bytes 393224 | tf_op jit(solution)/shard_map/ppermute | solution.py:325
  33.3 3.3 %copy-start.2 = (s32[64,128]{1,0:T(8,128)S(1)}, s32[64,128]{1,0:T(8,128)}, u32[]{:S(2)}) copy-start(s32[64,128]{1,0:T(8,128)} %valid.1) | copy-start | bytes 98308
  33.3 3.3 %copy-start.4 = (f32[512]{0:T(512)S(1)}, f32[512]{0:T(512)}, u32[]{:S(2)}) copy-start(f32[512]{0:T(512)} %param.17) | copy-start | bytes 6148
  33.3 3.3 %copy-start.5 = (s32[128]{0:T(128)S(1)}, s32[128]{0:T(128)}, u32[]{:S(2)}) copy-start(s32[128]{0:T(128)} %param.11) | copy-start | bytes 1540

commit v4 on v3

--- a/solution.py
+++ b/solution.py
@@ -9,7 +9,7 @@
 
 RIM = 48
 LANES = 128
-CHUNK = 256
+CHUNK = 512
 SHARPNESS = 40.0
 REACH = 10.0
 STRUCTS = 32
@@ -56,6 +56,28 @@
 
 def slot_group():
     return lax.axis_index("y") * 2 + lax.axis_index("zh")
+
+
+def pick_kernel(feat, rout, mixt, shard, sems):
+    core = lax.axis_index("k")
+
+    def take(weights):
+        moves = (
+            pltpu.make_async_copy(weights, shard.at[:, LANES:], sems.at[0]),
+            pltpu.make_async_copy(feat, shard.at[:, :LANES], sems.at[1]),
+        )
+        for move in moves:
+            move.start()
+        for move in moves:
+            move.wait()
+
+    @pl.when(core == 0)
+    def _():
+        take(rout)
+
+    @pl.when(core != 0)
+    def _():
+        take(mixt)
 
 
 def pack_kernel(here_shard, there_shard, out):
@@ -167,8 +189,9 @@
     weight = own_rows(valid).astype(F32)
     gdists = []
     onehots = []
-    for n in range(1024 // CHUNK):
-        per = CHUNK // LANES
+    per = CHUNK // LANES
+
+    def forward(n):
         row_of = iota((256, LANES), 0)
         onehot = jnp.concatenate(
             [
@@ -178,16 +201,25 @@
             axis=1,
         )
         onehots.append(onehot)
-        at = slice(n * CHUNK, (n + 1) * CHUNK)
         far = dot(table_f[...], onehot)
-        message = (far * radial[:, at]).astype(BF16)
-        mixed = dot(mix[...], message)
+        message = (far * radial[:, n * CHUNK : (n + 1) * CHUNK]).astype(BF16)
+        return far, dot(mix[...], message)
+
+    def backward(n, far, mixed):
         sig = sigmoid(mixed)
         slope = sig + mixed * sig * (1.0 - sig)
         wide = jnp.concatenate([scale[...]] * per, axis=1)
         gmix = (wide * slope).astype(BF16)
         gmsg = dot(mixt[...], gmix)
-        gdists.append(jnp.sum(gmsg * far * dradial[:, at], axis=0, keepdims=True))
+        kept = far * dradial[:, n * CHUNK : (n + 1) * CHUNK]
+        gdists.append(jnp.sum(gmsg * kept, axis=0, keepdims=True))
+
+    ahead = forward(0)
+    for n in range(1024 // CHUNK):
+        now = ahead
+        if n + 1 < 1024 // CHUNK:
+            ahead = forward(n + 1)
+        backward(n, *now)
     row8 = iota((8, LANES), 0)
     gdist = jnp.zeros((8, LANES), F32)
     for k in range(8):
@@ -309,8 +341,14 @@
     everyone = ("x", "zl", "k", "y", "zh")
     channels, edges = readout.shape[0], 8 * LANES
     rows = features.shape[0]
-    weights = jnp.where(lax.axis_index("k") == 0, radial_out, mixing.T)
-    shard = jnp.concatenate([features, weights], axis=1)
+    held = [pltpu.with_memory_space_constraint(a, pltpu.HBM) for a in (features, radial_out, mixing.T)]
+    shard = kernel(
+        pick_kernel,
+        [((rows, LANES + channels), BF16)],
+        4,
+        scratch=[pltpu.SemaphoreType.DMA((2,))],
+        space=pltpu.HBM,
+    )(*held)[0]
     shard_z = lax.ppermute(shard, "zh", [(0, 1), (1, 0)])
     packed = kernel(pack_kernel, [((4, 2 * rows, LANES + channels), BF16)], 4)(shard, shard_z)[0]
     gathered = lax.all_to_all(packed, "y", 0, 0, tiled=True)
@@ -333,7 +371,7 @@
     message = kernel(
         main_kernel,
         [((32, 8, LANES), F32)],
-        20,
+        32,
         scratch=[
             pltpu.VMEM((channels, 2 * LANES), BF16),
             pltpu.VMEM((channels, LANES), F32),

time: 73.4 us -> 71.7 us (0.977)
  other arithmetic: 1.59 us -> 0 us
    select_n x1 -> x0, other arithmetic: 0.86 us -> none  [local(): weights = jnp.where(lax.axis_index('k') == 0, radial_out, mixing.T)]
    pallas_call x6 -> x7, Pallas kernels: 7.23 us -> 7.11 us  [call(): pl.pallas_call(body, out_shape=[jax.ShapeDtypeStruct(shape, dtype) for sh...]
where the time goes in v4:
time: 71.7 us; the launch traced here: 71.4 us
  blocking collectives  44.3 us (62%)
  starting transfers between devices  13.4 us (19%)
  Pallas kernels  7.11 us (10%)
  waiting for transfers between devices  5.78 us (8%)
    all_to_all x1, blocking collectives, local(): got = lax.all_to_all(message, ('x', 'y', 'k'), 0, 0, tiled=True)  19.5 us
    all_to_all x1, blocking collectives, local(): gathered = lax.all_to_all(packed, 'y', 0, 0, tiled=True)  12.8 us
    all_to_all x1, blocking collectives, local(): got = lax.all_to_all(message, ('zl', 'zh'), 0, 0, tiled=True)  12 us
    ppermute x1, starting transfers between devices, local(): shard_z = lax.ppermute(shard, 'zh', [(0, 1), (1, 0)])  7.81 us
    pallas_call x7, Pallas kernels, call(): pl.pallas_call(body, out_shape=[jax.ShapeDtypeStruct(shape, dtype) for sh...  7.11 us
    ppermute x1, starting transfers between devices, local(): swapped = lax.ppermute(gathered, atoms, siblings)  3.24 us
    ppermute x1, waiting for transfers between devices, local(): cross = lax.ppermute(gathered[:, :, :LANES], everyone, crossing)  1.96 us
    ppermute x1, waiting for transfers between devices, local(): shard_z = lax.ppermute(shard, 'zh', [(0, 1), (1, 0)])  1.93 us
  transfers between devices with their start and end apart: 5, of which 4 were waited for; matrix products, arithmetic and copies ran while one was open for 0% of the time, Pallas kernels for 3%

profile of v4, /device:TPU:1, one launch (start us, length us, event | category | flops | bytes accessed | tf_op | source)
XLA Modules:
  0.0 71.4 jit_solution(16199325738170891435)
XLA Ops:
  0.6 0.9 %shard_map.104.here_shard = bf16[64,640]{1,0:T(8,128)(2,1)S(1)} custom-call(bf16[64,128]{1,0:T(8,128)(2,1)} %feat.1, bf16[64,512]{1,0:T(8,128)(2,1)} %rout.1, bf16[64,512]{1,0:T(8,128)(2,1)} %bitcast.5), custom_call_target="tpu_custom_call" | custom-call | flops 1000000000 | bytes 100000 | tf_op jit(solution)/shard_map/pallas_call | solution.py:24
  1.5 0.0 copy-start.3
  1.5 0.0 copy-start
  1.5 0.0 copy-start.1
  1.5 7.8 %collective-permute-start = (bf16[64,640]{1,0:T(8,128)(2,1)S(1)}, bf16[64,640]{1,0:T(8,128)(2,1)S(1)}, u32[]{:S(2)}, u32[]{:S(2)}) collective-permute-start(bf16[64,640]{1,0:T(8,128)(2,1)S(1)} %shard_map.104.here_shard), channel_id=1, source_target_pairs={{0,1},{1,0},{2,3},{3,2},{4,5},{5,4},{6,7},{7,6},{8,9},{9,8},{10,11... | collective-permute-start | bytes 245768 | tf_op jit(solution)/shard_map/ppermute | solution.py:352
  9.4 1.9 %collective-permute-done.there_shard = bf16[64,640]{1,0:T(8,128)(2,1)S(1)} collective-permute-done((bf16[64,640]{1,0:T(8,128)(2,1)S(1)}, bf16[64,640]{1,0:T(8,128)(2,1)S(1)}, u32[]{:S(2)}, u32[]{:S(2)}) %collective-permute-start) | collective-permute-done | bytes 81952 | tf_op jit(solution)/shard_map/ppermute | solution.py:352
  11.3 0.1 shard_map.105
  11.4 12.8 %all_to_all.15.gathered.own = bf16[4,128,640]{2,1,0:T(8,128)(2,1)S(1)} all-to-all(bf16[4,128,640]{2,1,0:T(8,128)(2,1)S(1)} %shard_map.105), channel_id=1, replica_groups=mesh['x'=4,'zl'=4,'k'=2,'y'=4,'zh'=2] {'y'}, dimensions={0} | all-to-all | bytes 1310720 | tf_op jit(solution)/shard_map/all_to_all | solution.py:354
  24.2 3.2 %collective-permute-start.1 = (bf16[4,128,640]{2,1,0:T(8,128)(2,1)S(1)}, bf16[4,128,640]{2,1,0:T(8,128)(2,1)S(1)}, u32[]{:S(2)}, u32[]{:S(2)}) collective-permute-start(bf16[4,128,640]{2,1,0:T(8,128)(2,1)S(1)} %all_to_all.15.gathered.own), channel_id=1, source_target_pairs={{0,8},{8,0},{16,24},{24,16},{32,40},{40,32},{48,56},{56,48},{64,72... | collective-permute-start | bytes 1966088 | tf_op jit(solution)/shard_map/ppermute | solution.py:364
  27.4 0.0 copy-done.3
  27.4 0.0 collective-permute-start.3
  27.4 1.1 %collective-permute-start.4 = (f32[3,128]{1,0:T(4,128)S(1)}, f32[3,128]{1,0:T(4,128)S(1)}, u32[]{:S(2)}, u32[]{:S(2)}) collective-permute-start(f32[3,128]{1,0:T(4,128)S(1)} %copy-done.3), channel_id=1, source_target_pairs={{8,16},{16,8},{9,17},{17,9},{10,18},{18,10},{11,19},{19,11},{12,20... | collective-permute-start | bytes 4616 | tf_op jit(solution)/shard_map/ppermute | solution.py:356
  28.5 0.6 collective-permute-done.3.sib
  29.1 1.3 %collective-permute-done.4.cross = f32[3,128]{1,0:T(4,128)S(1)} collective-permute-done((f32[3,128]{1,0:T(4,128)S(1)}, f32[3,128]{1,0:T(4,128)S(1)}, u32[]{:S(2)}, u32[]{:S(2)}) %collective-permute-start.4) | collective-permute-done | bytes 1568 | tf_op jit(solution)/shard_map/ppermute | solution.py:356
  30.4 0.0 copy-done
  30.4 0.0 copy-done.1
  30.4 1.1 %shard_map.106 = (bf16[512,1024]{1,0:T(8,128)(2,1)S(1)}, bf16[512,1024]{1,0:T(8,128)(2,1)S(1)}, f32[4,8,128]{2,1,0:T(8,128)S(1)}) custom-call(f32[3,128]{1,0:T(4,128)S(1)} %copy-done.3, f32[3,128]{1,0:T(4,128)S(1)} %collective-permute-done.3.sib, f32[3,128]{1,0:T(4,128)S(1)} %collective-permute-done.4.cross, s32[64,128]{1,0:T(8,128)S(1)} %copy-done.1, ...), custom_call_target="tpu_custom_call" | custom-call | flops 3000000000 | bytes 100000 | tf_op jit(solution)/shard_map/pallas_call | solution.py:24
  31.6 1.2 %collective-permute-start.2 = (bf16[4,128,128]{2,1,0:T(8,128)(2,1)S(1)}, bf16[4,128,128]{2,1,0:T(8,128)(2,1)S(1)}, u32[]{:S(2)}, u32[]{:S(2)}) collective-permute-start(bf16[4,128,128]{2,1,0:T(8,128)(2,1)S(1)} %slice.4), channel_id=1, source_target_pairs={{8,16},{16,8},{9,17},{17,9},{10,18},{18,10},{11,19},{19,11},{12,20... | collective-permute-start | bytes 393224 | tf_op jit(solution)/shard_map/ppermute | solution.py:363
  32.8 0.0 collective-permute-done.1.swapped.sib
  32.8 0.0 copy-start.2
  32.8 0.0 copy-start.4
  32.8 0.0 copy-start.5
  32.8 1.3 %shard_map.107 = (f32[512,1024]{1,0:T(8,128)S(1)}, f32[512,1024]{1,0:T(8,128)S(1)}, bf16[512,512]{1,0:T(8,128)(2,1)S(1)}, bf16[512,512]{1,0:T(8,128)(2,1)S(1)}) custom-call(bf16[4,128,640]{2,1,0:T(8,128)(2,1)S(1)} %all_to_all.15.gathered.own, bf16[4,128,640]{2,1,0:T(8,128)(2,1)S(1)} %collective-permute-done.1.swapped.sib, ...), custom_call_target="tpu_custom_call" | custom-call | flops 2000000000 | bytes 100000 | tf_op jit(solution)/shard_map/pallas_call | solution.py:24
  34.1 2.0 %collective-permute-done.2.cross = bf16[4,128,128]{2,1,0:T(8,128)(2,1)S(1)} collective-permute-done((bf16[4,128,128]{2,1,0:T(8,128)(2,1)S(1)}, bf16[4,128,128]{2,1,0:T(8,128)(2,1)S(1)}, u32[]{:S(2)}, u32[]{:S(2)}) %collective-permute-start.2) | collective-permute-done | bytes 131104 | tf_op jit(solution)/shard_map/ppermute | solution.py:363
  36.1 0.0 copy-done.2
  36.1 0.0 copy-done.4
  36.1 0.0 copy-done.5
  36.1 3.0 %shard_map.108 = f32[32,8,128]{2,1,0:T(8,128)S(1)} custom-call(bf16[4,128,640]{2,1,0:T(8,128)(2,1)S(1)} %all_to_all.15.gathered.own, bf16[4,128,640]{2,1,0:T(8,128)(2,1)S(1)} %collective-permute-done.1.swapped.sib, bf16[4,128,128]{2,1,0:T(8,128)(2,1)S(1)} %collective-permute-done.2.cross, f32[512,1024]{1,0:T(8,128)S(1)} %get-tuple-element.11.radial, ...), custom_call_target="tpu_custom_call" | custom-call | flops 4000000000 | bytes 100000 | tf_op jit(solution)/shard_map/pallas_call | solution.py:24
  39.1 19.5 %all_to_all.16.got = f32[32,8,128]{2,1,0:T(8,128)S(1)} all-to-all(f32[32,8,128]{2,1,0:T(8,128)S(1)} %shard_map.108), channel_id=1, replica_groups=mesh['x'=4,'zl'=4,'k'=2,'y'=4,'zh'=2] {'x','y','k'}, dimensions={0} | all-to-all | bytes 262144 | tf_op jit(solution)/shard_map/all_to_all | solution.py:394
  58.6 12.0 %all_to_all.17.got = f32[8,8,128]{2,1,0:T(8,128)S(1)} all-to-all(f32[8,8,128]{2,1,0:T(8,128)S(1)} %shard_map.109), channel_id=1, replica_groups=mesh['x'=4,'zl'=4,'k'=2,'y'=4,'zh'=2] {'zl','zh'}, dimensions={0} | all-to-all | bytes 65536 | tf_op jit(solution)/shard_map/all_to_all | solution.py:396
  70.7 0.8 %shard_map.110 = (f32[3,128]{1,0:T(4,128)}, f32[9,32]{1,0:T(8,128)}) custom-call(f32[8,8,128]{2,1,0:T(8,128)S(1)} %all_to_all.17.got), custom_call_target="tpu_custom_call" | custom-call | flops 1000000000 | bytes 100000 | tf_op jit(solution)/shard_map/pallas_call | solution.py:24
  (2 shorter events, 0.1 us)
Async XLA Ops:
  1.5 25.9 %copy-start.3 = (f32[3,128]{1,0:T(4,128)S(1)}, f32[3,128]{1,0:T(4,128)}, u32[]{:S(2)}) copy-start(f32[3,128]{1,0:T(4,128)} %pos.1) | copy-start | bytes 4612
  1.5 28.9 %copy-start = (bf16[512,128]{1,0:T(8,128)(2,1)S(1)}, bf16[512,128]{1,0:T(8,128)(2,1)}, u32[]{:S(2)}) copy-start(bf16[512,128]{1,0:T(8,128)(2,1)} %radial_in.1) | copy-start | bytes 393220
  1.5 28.9 %copy-start.1 = (s32[64,128]{1,0:T(8,128)S(1)}, s32[64,128]{1,0:T(8,128)}, u32[]{:S(2)}) copy-start(s32[64,128]{1,0:T(8,128)} %slots.3) | copy-start | bytes 98308
  1.5 9.7 %collective-permute-start = (bf16[64,640]{1,0:T(8,128)(2,1)S(1)}, bf16[64,640]{1,0:T(8,128)(2,1)S(1)}, u32[]{:S(2)}, u32[]{:S(2)}) collective-permute-start(bf16[64,640]{1,0:T(8,128)(2,1)S(1)} %shard_map.104.here_shard), channel_id=1, source_target_pairs={{0,1},{1,0},{2,3},{3,2},{4,5},{5,4},{6,7},{7,6},{8,9},{9,8},{10,11... | collective-permute-start | bytes 245768 | tf_op jit(solution)/shard_map/ppermute | solution.py:352
  24.2 8.7 %collective-permute-start.1 = (bf16[4,128,640]{2,1,0:T(8,128)(2,1)S(1)}, bf16[4,128,640]{2,1,0:T(8,128)(2,1)S(1)}, u32[]{:S(2)}, u32[]{:S(2)}) collective-permute-start(bf16[4,128,640]{2,1,0:T(8,128)(2,1)S(1)} %all_to_all.15.gathered.own), channel_id=1, source_target_pairs={{0,8},{8,0},{16,24},{24,16},{32,40},{40,32},{48,56},{56,48},{64,72... | collective-permute-start | bytes 1966088 | tf_op jit(solution)/shard_map/ppermute | solution.py:364
  27.4 1.7 %collective-permute-start.3 = (f32[3,128]{1,0:T(4,128)S(1)}, f32[3,128]{1,0:T(4,128)S(1)}, u32[]{:S(2)}, u32[]{:S(2)}) collective-permute-start(f32[3,128]{1,0:T(4,128)S(1)} %copy-done.3), channel_id=1, source_target_pairs={{0,8},{8,0},{16,24},{24,16},{32,40},{40,32},{48,56},{56,48},{64,72... | collective-permute-start | bytes 4616 | tf_op jit(solution)/shard_map/ppermute | solution.py:355
  27.4 3.0 %collective-permute-start.4 = (f32[3,128]{1,0:T(4,128)S(1)}, f32[3,128]{1,0:T(4,128)S(1)}, u32[]{:S(2)}, u32[]{:S(2)}) collective-permute-start(f32[3,128]{1,0:T(4,128)S(1)} %copy-done.3), channel_id=1, source_target_pairs={{8,16},{16,8},{9,17},{17,9},{10,18},{18,10},{11,19},{19,11},{12,20... | collective-permute-start | bytes 4616 | tf_op jit(solution)/shard_map/ppermute | solution.py:356
  31.6 4.5 %collective-permute-start.2 = (bf16[4,128,128]{2,1,0:T(8,128)(2,1)S(1)}, bf16[4,128,128]{2,1,0:T(8,128)(2,1)S(1)}, u32[]{:S(2)}, u32[]{:S(2)}) collective-permute-start(bf16[4,128,128]{2,1,0:T(8,128)(2,1)S(1)} %slice.4), channel_id=1, source_target_pairs={{8,16},{16,8},{9,17},{17,9},{10,18},{18,10},{11,19},{19,11},{12,20... | collective-permute-start | bytes 393224 | tf_op jit(solution)/shard_map/ppermute | solution.py:363
  32.8 3.3 %copy-start.2 = (s32[64,128]{1,0:T(8,128)S(1)}, s32[64,128]{1,0:T(8,128)}, u32[]{:S(2)}) copy-start(s32[64,128]{1,0:T(8,128)} %valid.1) | copy-start | bytes 98308
  32.8 3.3 %copy-start.4 = (f32[512]{0:T(512)S(1)}, f32[512]{0:T(512)}, u32[]{:S(2)}) copy-start(f32[512]{0:T(512)} %param.17) | copy-start | bytes 6148
  32.8 3.3 %copy-start.5 = (s32[128]{0:T(128)S(1)}, s32[128]{0:T(128)}, u32[]{:S(2)}) copy-start(s32[128]{0:T(128)} %param.11) | copy-start | bytes 1540

commit v5 on v4

--- a/solution.py
+++ b/solution.py
@@ -44,6 +44,15 @@
 
 def dot_t(a, b):
     return lax.dot_general(a, b, (((1,), (1,)), ((), ())), preferred_element_type=F32)
+
+
+def exact_dot_t(a, b):
+    parts, rest = [], a
+    for _ in range(3):
+        parts.append(rest.astype(BF16).astype(F32))
+        rest = rest - parts[-1]
+    sums = dot_t(jnp.concatenate(parts, axis=0).astype(BF16), b)
+    return sums[0:8] + sums[8:16] + sums[16:24]
 
 
 def sigmoid(v):
@@ -234,18 +243,15 @@
         return jnp.broadcast_to(jnp.sum(v, axis=0, keepdims=True), (8, LANES))
 
     zero = jnp.zeros((8, LANES), F32)
-    acc = jnp.zeros((8, 256), F32)
+    blocks = []
     for k in range(8):
         rows = zero
         for p in range(3):
             rows = jnp.where(row8 == p, jnp.broadcast_to(gvec[p][k : k + 1, :], (8, LANES)), rows)
-        per = CHUNK // LANES
-        hot = onehots[k // per][:, (k % per) * LANES : (k % per + 1) * LANES]
-        rest = rows
-        for _ in range(3):
-            part = rest.astype(BF16)
-            acc = acc + dot_t(part, hot)
-            rest = rest - part.astype(F32)
+        blocks.append(rows)
+    acc = jnp.zeros((8, 256), F32)
+    for n, hot in enumerate(onehots):
+        acc = acc + exact_dot_t(jnp.concatenate(blocks[n * per : (n + 1) * per], axis=1), hot)
     mine, ring = -acc[:, :LANES], -acc[:, LANES:]
     for p in range(3):
         mine = mine + jnp.where(row8 == p, total(gvec[p]), 0.0)
@@ -255,12 +261,7 @@
         vir = jnp.where(row8 == j, total(vecs[p] * gvec[q]), vir)
     struct = iota((LANES, LANES), 0) & (STRUCTS - 1)
     member = (struct == jnp.broadcast_to(ids[...], (LANES, LANES))).astype(F32).astype(BF16)
-    spread = jnp.zeros((8, LANES), F32)
-    rest = vir
-    for _ in range(3):
-        part = rest.astype(BF16)
-        spread = spread + dot_t(part, member)
-        rest = rest - part.astype(F32)
+    spread = exact_dot_t(vir, member)
     lane8 = iota((8, LANES), 1)
     picked = jnp.where((lane8 >> 5) == (row8 & 3), spread, 0.0)
     first_row = total(jnp.where(row8 < 4, picked, 0.0))

time: 71.7 us -> 70.9 us (0.989)
  Pallas kernels: 7.11 us -> 6.37 us
    pallas_call x7, Pallas kernels: 7.11 us -> 6.37 us  [call(): pl.pallas_call(body, out_shape=[jax.ShapeDtypeStruct(shape, dtype) for sh...]
where the time goes in v5:
time: 70.9 us; the launch traced here: 70.7 us
  blocking collectives  44.4 us (63%)
  starting transfers between devices  13.4 us (19%)
  Pallas kernels  6.37 us (9%)
  waiting for transfers between devices  5.78 us (8%)
  between operations  0.71 us (1%)
    all_to_all x1, blocking collectives, local(): got = lax.all_to_all(message, ('x', 'y', 'k'), 0, 0, tiled=True)  19.5 us
    all_to_all x1, blocking collectives, local(): gathered = lax.all_to_all(packed, 'y', 0, 0, tiled=True)  12.8 us
    all_to_all x1, blocking collectives, local(): got = lax.all_to_all(message, ('zl', 'zh'), 0, 0, tiled=True)  12 us
    ppermute x1, starting transfers between devices, local(): shard_z = lax.ppermute(shard, 'zh', [(0, 1), (1, 0)])  7.81 us
    pallas_call x7, Pallas kernels, call(): pl.pallas_call(body, out_shape=[jax.ShapeDtypeStruct(shape, dtype) for sh...  6.37 us
    ppermute x1, starting transfers between devices, local(): swapped = lax.ppermute(gathered, atoms, siblings)  3.24 us
    ppermute x1, waiting for transfers between devices, local(): cross = lax.ppermute(gathered[:, :, :LANES], everyone, crossing)  1.96 us
    ppermute x1, waiting for transfers between devices, local(): shard_z = lax.ppermute(shard, 'zh', [(0, 1), (1, 0)])  1.93 us
  transfers between devices with their start and end apart: 5, of which 4 were waited for; matrix products, arithmetic and copies ran while one was open for 0% of the time, Pallas kernels for 3%

profile of v5, /device:TPU:1, one launch (start us, length us, event | category | flops | bytes accessed | tf_op | source)
XLA Modules:
  0.0 70.7 jit_solution(3769963488226369550)
XLA Ops:
  0.6 0.9 %shard_map.104.here_shard = bf16[64,640]{1,0:T(8,128)(2,1)S(1)} custom-call(bf16[64,128]{1,0:T(8,128)(2,1)} %feat.1, bf16[64,512]{1,0:T(8,128)(2,1)} %rout.1, bf16[64,512]{1,0:T(8,128)(2,1)} %bitcast.5), custom_call_target="tpu_custom_call" | custom-call | flops 1000000000 | bytes 100000 | tf_op jit(solution)/shard_map/pallas_call | solution.py:24
  1.5 0.0 copy-start.3
  1.5 0.0 copy-start
  1.5 0.0 copy-start.1
  1.5 7.8 %collective-permute-start = (bf16[64,640]{1,0:T(8,128)(2,1)S(1)}, bf16[64,640]{1,0:T(8,128)(2,1)S(1)}, u32[]{:S(2)}, u32[]{:S(2)}) collective-permute-start(bf16[64,640]{1,0:T(8,128)(2,1)S(1)} %shard_map.104.here_shard), channel_id=1, source_target_pairs={{0,1},{1,0},{2,3},{3,2},{4,5},{5,4},{6,7},{7,6},{8,9},{9,8},{10,11... | collective-permute-start | bytes 245768 | tf_op jit(solution)/shard_map/ppermute | solution.py:353
  9.4 1.9 %collective-permute-done.there_shard = bf16[64,640]{1,0:T(8,128)(2,1)S(1)} collective-permute-done((bf16[64,640]{1,0:T(8,128)(2,1)S(1)}, bf16[64,640]{1,0:T(8,128)(2,1)S(1)}, u32[]{:S(2)}, u32[]{:S(2)}) %collective-permute-start) | collective-permute-done | bytes 81952 | tf_op jit(solution)/shard_map/ppermute | solution.py:353
  11.3 0.1 shard_map.105
  11.4 12.8 %all_to_all.15.gathered.own = bf16[4,128,640]{2,1,0:T(8,128)(2,1)S(1)} all-to-all(bf16[4,128,640]{2,1,0:T(8,128)(2,1)S(1)} %shard_map.105), channel_id=1, replica_groups=mesh['x'=4,'zl'=4,'k'=2,'y'=4,'zh'=2] {'y'}, dimensions={0} | all-to-all | bytes 1310720 | tf_op jit(solution)/shard_map/all_to_all | solution.py:355
  24.2 3.2 %collective-permute-start.1 = (bf16[4,128,640]{2,1,0:T(8,128)(2,1)S(1)}, bf16[4,128,640]{2,1,0:T(8,128)(2,1)S(1)}, u32[]{:S(2)}, u32[]{:S(2)}) collective-permute-start(bf16[4,128,640]{2,1,0:T(8,128)(2,1)S(1)} %all_to_all.15.gathered.own), channel_id=1, source_target_pairs={{0,8},{8,0},{16,24},{24,16},{32,40},{40,32},{48,56},{56,48},{64,72... | collective-permute-start | bytes 1966088 | tf_op jit(solution)/shard_map/ppermute | solution.py:365
  27.4 0.0 copy-done.3
  27.4 0.0 collective-permute-start.3
  27.4 1.1 %collective-permute-start.4 = (f32[3,128]{1,0:T(4,128)S(1)}, f32[3,128]{1,0:T(4,128)S(1)}, u32[]{:S(2)}, u32[]{:S(2)}) collective-permute-start(f32[3,128]{1,0:T(4,128)S(1)} %copy-done.3), channel_id=1, source_target_pairs={{8,16},{16,8},{9,17},{17,9},{10,18},{18,10},{11,19},{19,11},{12,20... | collective-permute-start | bytes 4616 | tf_op jit(solution)/shard_map/ppermute | solution.py:357
  28.5 0.6 collective-permute-done.3.sib
  29.1 1.3 %collective-permute-done.4.cross = f32[3,128]{1,0:T(4,128)S(1)} collective-permute-done((f32[3,128]{1,0:T(4,128)S(1)}, f32[3,128]{1,0:T(4,128)S(1)}, u32[]{:S(2)}, u32[]{:S(2)}) %collective-permute-start.4) | collective-permute-done | bytes 1568 | tf_op jit(solution)/shard_map/ppermute | solution.py:357
  30.4 0.0 copy-done
  30.4 0.0 copy-done.1
  30.4 1.1 %shard_map.106 = (bf16[512,1024]{1,0:T(8,128)(2,1)S(1)}, bf16[512,1024]{1,0:T(8,128)(2,1)S(1)}, f32[4,8,128]{2,1,0:T(8,128)S(1)}) custom-call(f32[3,128]{1,0:T(4,128)S(1)} %copy-done.3, f32[3,128]{1,0:T(4,128)S(1)} %collective-permute-done.3.sib, f32[3,128]{1,0:T(4,128)S(1)} %collective-permute-done.4.cross, s32[64,128]{1,0:T(8,128)S(1)} %copy-done.1, ...), custom_call_target="tpu_custom_call" | custom-call | flops 3000000000 | bytes 100000 | tf_op jit(solution)/shard_map/pallas_call | solution.py:24
  31.6 1.2 %collective-permute-start.2 = (bf16[4,128,128]{2,1,0:T(8,128)(2,1)S(1)}, bf16[4,128,128]{2,1,0:T(8,128)(2,1)S(1)}, u32[]{:S(2)}, u32[]{:S(2)}) collective-permute-start(bf16[4,128,128]{2,1,0:T(8,128)(2,1)S(1)} %slice.4), channel_id=1, source_target_pairs={{8,16},{16,8},{9,17},{17,9},{10,18},{18,10},{11,19},{19,11},{12,20... | collective-permute-start | bytes 393224 | tf_op jit(solution)/shard_map/ppermute | solution.py:364
  32.8 0.0 collective-permute-done.1.swapped.sib
  32.8 0.0 copy-start.2
  32.8 0.0 copy-start.4
  32.8 0.0 copy-start.5
  32.8 1.3 %shard_map.107 = (f32[512,1024]{1,0:T(8,128)S(1)}, f32[512,1024]{1,0:T(8,128)S(1)}, bf16[512,512]{1,0:T(8,128)(2,1)S(1)}, bf16[512,512]{1,0:T(8,128)(2,1)S(1)}) custom-call(bf16[4,128,640]{2,1,0:T(8,128)(2,1)S(1)} %all_to_all.15.gathered.own, bf16[4,128,640]{2,1,0:T(8,128)(2,1)S(1)} %collective-permute-done.1.swapped.sib, ...), custom_call_target="tpu_custom_call" | custom-call | flops 2000000000 | bytes 100000 | tf_op jit(solution)/shard_map/pallas_call | solution.py:24
  34.1 2.0 %collective-permute-done.2.cross = bf16[4,128,128]{2,1,0:T(8,128)(2,1)S(1)} collective-permute-done((bf16[4,128,128]{2,1,0:T(8,128)(2,1)S(1)}, bf16[4,128,128]{2,1,0:T(8,128)(2,1)S(1)}, u32[]{:S(2)}, u32[]{:S(2)}) %collective-permute-start.2) | collective-permute-done | bytes 131104 | tf_op jit(solution)/shard_map/ppermute | solution.py:364
  36.1 0.0 copy-done.2
  36.1 0.0 copy-done.4
  36.1 0.0 copy-done.5
  36.1 2.2 %shard_map.108 = f32[32,8,128]{2,1,0:T(8,128)S(1)} custom-call(bf16[4,128,640]{2,1,0:T(8,128)(2,1)S(1)} %all_to_all.15.gathered.own, bf16[4,128,640]{2,1,0:T(8,128)(2,1)S(1)} %collective-permute-done.1.swapped.sib, bf16[4,128,128]{2,1,0:T(8,128)(2,1)S(1)} %collective-permute-done.2.cross, f32[512,1024]{1,0:T(8,128)S(1)} %get-tuple-element.11.radial, ...), custom_call_target="tpu_custom_call" | custom-call | flops 4000000000 | bytes 100000 | tf_op jit(solution)/shard_map/pallas_call | solution.py:24
  38.3 19.5 %all_to_all.16.got = f32[32,8,128]{2,1,0:T(8,128)S(1)} all-to-all(f32[32,8,128]{2,1,0:T(8,128)S(1)} %shard_map.108), channel_id=1, replica_groups=mesh['x'=4,'zl'=4,'k'=2,'y'=4,'zh'=2] {'x','y','k'}, dimensions={0} | all-to-all | bytes 262144 | tf_op jit(solution)/shard_map/all_to_all | solution.py:395
  57.9 12.0 %all_to_all.17.got = f32[8,8,128]{2,1,0:T(8,128)S(1)} all-to-all(f32[8,8,128]{2,1,0:T(8,128)S(1)} %shard_map.109), channel_id=1, replica_groups=mesh['x'=4,'zl'=4,'k'=2,'y'=4,'zh'=2] {'zl','zh'}, dimensions={0} | all-to-all | bytes 65536 | tf_op jit(solution)/shard_map/all_to_all | solution.py:397
  69.9 0.8 %shard_map.110 = (f32[3,128]{1,0:T(4,128)}, f32[9,32]{1,0:T(8,128)}) custom-call(f32[8,8,128]{2,1,0:T(8,128)S(1)} %all_to_all.17.got), custom_call_target="tpu_custom_call" | custom-call | flops 1000000000 | bytes 100000 | tf_op jit(solution)/shard_map/pallas_call | solution.py:24
  (2 shorter events, 0.1 us)
Async XLA Ops:
  1.5 25.9 %copy-start.3 = (f32[3,128]{1,0:T(4,128)S(1)}, f32[3,128]{1,0:T(4,128)}, u32[]{:S(2)}) copy-start(f32[3,128]{1,0:T(4,128)} %pos.1) | copy-start | bytes 4612
  1.5 28.9 %copy-start = (bf16[512,128]{1,0:T(8,128)(2,1)S(1)}, bf16[512,128]{1,0:T(8,128)(2,1)}, u32[]{:S(2)}) copy-start(bf16[512,128]{1,0:T(8,128)(2,1)} %radial_in.1) | copy-start | bytes 393220
  1.5 28.9 %copy-start.1 = (s32[64,128]{1,0:T(8,128)S(1)}, s32[64,128]{1,0:T(8,128)}, u32[]{:S(2)}) copy-start(s32[64,128]{1,0:T(8,128)} %slots.3) | copy-start | bytes 98308
  1.5 9.7 %collective-permute-start = (bf16[64,640]{1,0:T(8,128)(2,1)S(1)}, bf16[64,640]{1,0:T(8,128)(2,1)S(1)}, u32[]{:S(2)}, u32[]{:S(2)}) collective-permute-start(bf16[64,640]{1,0:T(8,128)(2,1)S(1)} %shard_map.104.here_shard), channel_id=1, source_target_pairs={{0,1},{1,0},{2,3},{3,2},{4,5},{5,4},{6,7},{7,6},{8,9},{9,8},{10,11... | collective-permute-start | bytes 245768 | tf_op jit(solution)/shard_map/ppermute | solution.py:353
  24.2 8.7 %collective-permute-start.1 = (bf16[4,128,640]{2,1,0:T(8,128)(2,1)S(1)}, bf16[4,128,640]{2,1,0:T(8,128)(2,1)S(1)}, u32[]{:S(2)}, u32[]{:S(2)}) collective-permute-start(bf16[4,128,640]{2,1,0:T(8,128)(2,1)S(1)} %all_to_all.15.gathered.own), channel_id=1, source_target_pairs={{0,8},{8,0},{16,24},{24,16},{32,40},{40,32},{48,56},{56,48},{64,72... | collective-permute-start | bytes 1966088 | tf_op jit(solution)/shard_map/ppermute | solution.py:365
  27.4 1.7 %collective-permute-start.3 = (f32[3,128]{1,0:T(4,128)S(1)}, f32[3,128]{1,0:T(4,128)S(1)}, u32[]{:S(2)}, u32[]{:S(2)}) collective-permute-start(f32[3,128]{1,0:T(4,128)S(1)} %copy-done.3), channel_id=1, source_target_pairs={{0,8},{8,0},{16,24},{24,16},{32,40},{40,32},{48,56},{56,48},{64,72... | collective-permute-start | bytes 4616 | tf_op jit(solution)/shard_map/ppermute | solution.py:356
  27.4 3.0 %collective-permute-start.4 = (f32[3,128]{1,0:T(4,128)S(1)}, f32[3,128]{1,0:T(4,128)S(1)}, u32[]{:S(2)}, u32[]{:S(2)}) collective-permute-start(f32[3,128]{1,0:T(4,128)S(1)} %copy-done.3), channel_id=1, source_target_pairs={{8,16},{16,8},{9,17},{17,9},{10,18},{18,10},{11,19},{19,11},{12,20... | collective-permute-start | bytes 4616 | tf_op jit(solution)/shard_map/ppermute | solution.py:357
  31.6 4.5 %collective-permute-start.2 = (bf16[4,128,128]{2,1,0:T(8,128)(2,1)S(1)}, bf16[4,128,128]{2,1,0:T(8,128)(2,1)S(1)}, u32[]{:S(2)}, u32[]{:S(2)}) collective-permute-start(bf16[4,128,128]{2,1,0:T(8,128)(2,1)S(1)} %slice.4), channel_id=1, source_target_pairs={{8,16},{16,8},{9,17},{17,9},{10,18},{18,10},{11,19},{19,11},{12,20... | collective-permute-start | bytes 393224 | tf_op jit(solution)/shard_map/ppermute | solution.py:364
  32.8 3.3 %copy-start.2 = (s32[64,128]{1,0:T(8,128)S(1)}, s32[64,128]{1,0:T(8,128)}, u32[]{:S(2)}) copy-start(s32[64,128]{1,0:T(8,128)} %valid.1) | copy-start | bytes 98308
  32.8 3.3 %copy-start.4 = (f32[512]{0:T(512)S(1)}, f32[512]{0:T(512)}, u32[]{:S(2)}) copy-start(f32[512]{0:T(512)} %param.17) | copy-start | bytes 6148
  32.8 3.3 %copy-start.5 = (s32[128]{0:T(128)S(1)}, s32[128]{0:T(128)}, u32[]{:S(2)}) copy-start(s32[128]{0:T(128)} %param.11) | copy-start | bytes 1540

commit v6 on v5

--- a/solution.py
+++ b/solution.py
@@ -53,10 +53,6 @@
         rest = rest - parts[-1]
     sums = dot_t(jnp.concatenate(parts, axis=0).astype(BF16), b)
     return sums[0:8] + sums[8:16] + sums[16:24]
-
-
-def sigmoid(v):
-    return 0.5 + 0.5 * jnp.tanh(0.5 * v)
 
 
 def where_am_i():
@@ -141,19 +137,19 @@
     geo[3] = dist
     count = radial_in.shape[1]
     centers = iota((count, LANES), 0).astype(F32) * (REACH / count)
-    weights = radial_in[...]
+    weights = (radial_in[...].astype(F32) * 0.5).astype(BF16)
     for k in range(8):
         offset = jnp.broadcast_to(dist[k : k + 1, :], (count, LANES)) - centers
         bump = jnp.exp(-SHARPNESS * offset * offset)
         slope = (-2.0 * SHARPNESS * offset * bump).astype(BF16)
         both = jnp.concatenate([bump.astype(BF16), slope], axis=1)
         pre2 = dot(weights, both)
-        pre, dpre = pre2[:, :LANES], pre2[:, LANES:]
-        sig = sigmoid(pre)
-        silu = pre * sig
+        half, dhalf = pre2[:, :LANES], pre2[:, LANES:]
+        turn = jnp.tanh(half)
+        rise = 1.0 + turn
         at = slice(k * LANES, (k + 1) * LANES)
-        hidden[:, at] = silu.astype(BF16)
-        dhidden[:, at] = ((sig + silu * (1.0 - sig)) * dpre).astype(BF16)
+        hidden[:, at] = (half * rise).astype(BF16)
+        dhidden[:, at] = (rise * (1.0 + half * (1.0 - turn)) * dhalf).astype(BF16)
 
 
 def radial_kernel(gathered, swapped, hidden, dhidden, radial, dradial, mix, mixt):
@@ -168,7 +164,7 @@
             dradial[:, at] = dot(weights, dhidden[:, at])
         turned = w_mixt[:, :, LANES:].reshape(channels, channels)
         mixt[...] = turned
-        mix[...] = turned.T
+        mix[...] = (turned.astype(F32) * 0.5).astype(BF16).T
 
     @pl.when(core == 0)
     def _():
@@ -192,7 +188,7 @@
     table_f[:, LANES:] = halo_of(core, sib_f, cross_f, lane)
     turned = jnp.concatenate([readout[...]] * 2, axis=0).T
     for j in range(4):
-        scale[j * LANES : (j + 1) * LANES, :] = jnp.broadcast_to(turned[:, j : j + 1], (LANES, LANES))
+        scale[j * LANES : (j + 1) * LANES, :] = jnp.broadcast_to(0.5 * turned[:, j : j + 1], (LANES, LANES))
 
     idx = slot_index(slots)
     weight = own_rows(valid).astype(F32)
@@ -215,8 +211,8 @@
         return far, dot(mix[...], message)
 
     def backward(n, far, mixed):
-        sig = sigmoid(mixed)
-        slope = sig + mixed * sig * (1.0 - sig)
+        turn = jnp.tanh(mixed)
+        slope = (1.0 + turn) * (1.0 + mixed * (1.0 - turn))
         wide = jnp.concatenate([scale[...]] * per, axis=1)
         gmix = (wide * slope).astype(BF16)
         gmsg = dot(mixt[...], gmix)

time: 70.9 us -> 70.9 us (level)
  no operation moved by 1% of the time
where the time goes in v6:
time: 70.9 us; the launch traced here: 70.6 us
  blocking collectives  44.3 us (62%)
  starting transfers between devices  13.4 us (19%)
  Pallas kernels  6.33 us (9%)
  waiting for transfers between devices  5.78 us (8%)
  between operations  0.71 us (1%)
    all_to_all x1, blocking collectives, local(): got = lax.all_to_all(message, ('x', 'y', 'k'), 0, 0, tiled=True)  19.5 us
    all_to_all x1, blocking collectives, local(): gathered = lax.all_to_all(packed, 'y', 0, 0, tiled=True)  12.8 us
    all_to_all x1, blocking collectives, local(): got = lax.all_to_all(message, ('zl', 'zh'), 0, 0, tiled=True)  12 us
    ppermute x1, starting transfers between devices, local(): shard_z = lax.ppermute(shard, 'zh', [(0, 1), (1, 0)])  7.81 us
    pallas_call x7, Pallas kernels, call(): pl.pallas_call(body, out_shape=[jax.ShapeDtypeStruct(shape, dtype) for sh...  6.33 us
    ppermute x1, starting transfers between devices, local(): swapped = lax.ppermute(gathered, atoms, siblings)  3.24 us
    ppermute x1, waiting for transfers between devices, local(): cross = lax.ppermute(gathered[:, :, :LANES], everyone, crossing)  1.97 us
    ppermute x1, waiting for transfers between devices, local(): shard_z = lax.ppermute(shard, 'zh', [(0, 1), (1, 0)])  1.93 us
  transfers between devices with their start and end apart: 5, of which 4 were waited for; matrix products, arithmetic and copies ran while one was open for 0% of the time, Pallas kernels for 3%

profile of v6, /device:TPU:1, one launch (start us, length us, event | category | flops | bytes accessed | tf_op | source)
XLA Modules:
  0.0 70.6 jit_solution(632392990631444536)
XLA Ops:
  0.6 0.9 %shard_map.104.here_shard = bf16[64,640]{1,0:T(8,128)(2,1)S(1)} custom-call(bf16[64,128]{1,0:T(8,128)(2,1)} %feat.1, bf16[64,512]{1,0:T(8,128)(2,1)} %rout.1, bf16[64,512]{1,0:T(8,128)(2,1)} %bitcast.5), custom_call_target="tpu_custom_call" | custom-call | flops 1000000000 | bytes 100000 | tf_op jit(solution)/shard_map/pallas_call | solution.py:24
  1.5 0.0 copy-start.3
  1.5 0.0 copy-start
  1.5 0.0 copy-start.1
  1.5 7.8 %collective-permute-start = (bf16[64,640]{1,0:T(8,128)(2,1)S(1)}, bf16[64,640]{1,0:T(8,128)(2,1)S(1)}, u32[]{:S(2)}, u32[]{:S(2)}) collective-permute-start(bf16[64,640]{1,0:T(8,128)(2,1)S(1)} %shard_map.104.here_shard), channel_id=1, source_target_pairs={{0,1},{1,0},{2,3},{3,2},{4,5},{5,4},{6,7},{7,6},{8,9},{9,8},{10,11... | collective-permute-start | bytes 245768 | tf_op jit(solution)/shard_map/ppermute | solution.py:349
  9.4 1.9 %collective-permute-done.there_shard = bf16[64,640]{1,0:T(8,128)(2,1)S(1)} collective-permute-done((bf16[64,640]{1,0:T(8,128)(2,1)S(1)}, bf16[64,640]{1,0:T(8,128)(2,1)S(1)}, u32[]{:S(2)}, u32[]{:S(2)}) %collective-permute-start) | collective-permute-done | bytes 81952 | tf_op jit(solution)/shard_map/ppermute | solution.py:349
  11.3 0.1 shard_map.105
  11.4 12.8 %all_to_all.15.gathered.own = bf16[4,128,640]{2,1,0:T(8,128)(2,1)S(1)} all-to-all(bf16[4,128,640]{2,1,0:T(8,128)(2,1)S(1)} %shard_map.105), channel_id=1, replica_groups=mesh['x'=4,'zl'=4,'k'=2,'y'=4,'zh'=2] {'y'}, dimensions={0} | all-to-all | bytes 1310720 | tf_op jit(solution)/shard_map/all_to_all | solution.py:351
  24.2 3.2 %collective-permute-start.1 = (bf16[4,128,640]{2,1,0:T(8,128)(2,1)S(1)}, bf16[4,128,640]{2,1,0:T(8,128)(2,1)S(1)}, u32[]{:S(2)}, u32[]{:S(2)}) collective-permute-start(bf16[4,128,640]{2,1,0:T(8,128)(2,1)S(1)} %all_to_all.15.gathered.own), channel_id=1, source_target_pairs={{0,8},{8,0},{16,24},{24,16},{32,40},{40,32},{48,56},{56,48},{64,72... | collective-permute-start | bytes 1966088 | tf_op jit(solution)/shard_map/ppermute | solution.py:361
  27.4 0.0 copy-done.3
  27.4 0.0 collective-permute-start.3
  27.4 1.1 %collective-permute-start.4 = (f32[3,128]{1,0:T(4,128)S(1)}, f32[3,128]{1,0:T(4,128)S(1)}, u32[]{:S(2)}, u32[]{:S(2)}) collective-permute-start(f32[3,128]{1,0:T(4,128)S(1)} %copy-done.3), channel_id=1, source_target_pairs={{8,16},{16,8},{9,17},{17,9},{10,18},{18,10},{11,19},{19,11},{12,20... | collective-permute-start | bytes 4616 | tf_op jit(solution)/shard_map/ppermute | solution.py:353
  28.5 0.6 collective-permute-done.3.sib
  29.1 1.3 %collective-permute-done.4.cross = f32[3,128]{1,0:T(4,128)S(1)} collective-permute-done((f32[3,128]{1,0:T(4,128)S(1)}, f32[3,128]{1,0:T(4,128)S(1)}, u32[]{:S(2)}, u32[]{:S(2)}) %collective-permute-start.4) | collective-permute-done | bytes 1568 | tf_op jit(solution)/shard_map/ppermute | solution.py:353
  30.4 0.0 copy-done
  30.4 0.0 copy-done.1
  30.4 1.1 %shard_map.106 = (bf16[512,1024]{1,0:T(8,128)(2,1)S(1)}, bf16[512,1024]{1,0:T(8,128)(2,1)S(1)}, f32[4,8,128]{2,1,0:T(8,128)S(1)}) custom-call(f32[3,128]{1,0:T(4,128)S(1)} %copy-done.3, f32[3,128]{1,0:T(4,128)S(1)} %collective-permute-done.3.sib, f32[3,128]{1,0:T(4,128)S(1)} %collective-permute-done.4.cross, s32[64,128]{1,0:T(8,128)S(1)} %copy-done.1, ...), custom_call_target="tpu_custom_call" | custom-call | flops 3000000000 | bytes 100000 | tf_op jit(solution)/shard_map/pallas_call | solution.py:24
  31.5 1.2 %collective-permute-start.2 = (bf16[4,128,128]{2,1,0:T(8,128)(2,1)S(1)}, bf16[4,128,128]{2,1,0:T(8,128)(2,1)S(1)}, u32[]{:S(2)}, u32[]{:S(2)}) collective-permute-start(bf16[4,128,128]{2,1,0:T(8,128)(2,1)S(1)} %slice.4), channel_id=1, source_target_pairs={{8,16},{16,8},{9,17},{17,9},{10,18},{18,10},{11,19},{19,11},{12,20... | collective-permute-start | bytes 393224 | tf_op jit(solution)/shard_map/ppermute | solution.py:360
  32.7 0.0 collective-permute-done.1.swapped.sib
  32.7 0.0 copy-start.2
  32.8 0.0 copy-start.4
  32.8 0.0 copy-start.5
  32.8 1.3 %shard_map.107 = (f32[512,1024]{1,0:T(8,128)S(1)}, f32[512,1024]{1,0:T(8,128)S(1)}, bf16[512,512]{1,0:T(8,128)(2,1)S(1)}, bf16[512,512]{1,0:T(8,128)(2,1)S(1)}) custom-call(bf16[4,128,640]{2,1,0:T(8,128)(2,1)S(1)} %all_to_all.15.gathered.own, bf16[4,128,640]{2,1,0:T(8,128)(2,1)S(1)} %collective-permute-done.1.swapped.sib, ...), custom_call_target="tpu_custom_call" | custom-call | flops 2000000000 | bytes 100000 | tf_op jit(solution)/shard_map/pallas_call | solution.py:24
  34.0 2.0 %collective-permute-done.2.cross = bf16[4,128,128]{2,1,0:T(8,128)(2,1)S(1)} collective-permute-done((bf16[4,128,128]{2,1,0:T(8,128)(2,1)S(1)}, bf16[4,128,128]{2,1,0:T(8,128)(2,1)S(1)}, u32[]{:S(2)}, u32[]{:S(2)}) %collective-permute-start.2) | collective-permute-done | bytes 131104 | tf_op jit(solution)/shard_map/ppermute | solution.py:360
  36.0 0.0 copy-done.2
  36.0 0.0 copy-done.4
  36.0 0.0 copy-done.5
  36.0 2.3 %shard_map.108 = f32[32,8,128]{2,1,0:T(8,128)S(1)} custom-call(bf16[4,128,640]{2,1,0:T(8,128)(2,1)S(1)} %all_to_all.15.gathered.own, bf16[4,128,640]{2,1,0:T(8,128)(2,1)S(1)} %collective-permute-done.1.swapped.sib, bf16[4,128,128]{2,1,0:T(8,128)(2,1)S(1)} %collective-permute-done.2.cross, f32[512,1024]{1,0:T(8,128)S(1)} %get-tuple-element.11.radial, ...), custom_call_target="tpu_custom_call" | custom-call | flops 4000000000 | bytes 100000 | tf_op jit(solution)/shard_map/pallas_call | solution.py:24
  38.3 19.5 %all_to_all.16.got = f32[32,8,128]{2,1,0:T(8,128)S(1)} all-to-all(f32[32,8,128]{2,1,0:T(8,128)S(1)} %shard_map.108), channel_id=1, replica_groups=mesh['x'=4,'zl'=4,'k'=2,'y'=4,'zh'=2] {'x','y','k'}, dimensions={0} | all-to-all | bytes 262144 | tf_op jit(solution)/shard_map/all_to_all | solution.py:391
  57.8 12.0 %all_to_all.17.got = f32[8,8,128]{2,1,0:T(8,128)S(1)} all-to-all(f32[8,8,128]{2,1,0:T(8,128)S(1)} %shard_map.109), channel_id=1, replica_groups=mesh['x'=4,'zl'=4,'k'=2,'y'=4,'zh'=2] {'zl','zh'}, dimensions={0} | all-to-all | bytes 65536 | tf_op jit(solution)/shard_map/all_to_all | solution.py:393
  69.9 0.8 %shard_map.110 = (f32[3,128]{1,0:T(4,128)}, f32[9,32]{1,0:T(8,128)}) custom-call(f32[8,8,128]{2,1,0:T(8,128)S(1)} %all_to_all.17.got), custom_call_target="tpu_custom_call" | custom-call | flops 1000000000 | bytes 100000 | tf_op jit(solution)/shard_map/pallas_call | solution.py:24
  (2 shorter events, 0.1 us)
Async XLA Ops:
  1.5 25.9 %copy-start.3 = (f32[3,128]{1,0:T(4,128)S(1)}, f32[3,128]{1,0:T(4,128)}, u32[]{:S(2)}) copy-start(f32[3,128]{1,0:T(4,128)} %pos.1) | copy-start | bytes 4612
  1.5 28.9 %copy-start = (bf16[512,128]{1,0:T(8,128)(2,1)S(1)}, bf16[512,128]{1,0:T(8,128)(2,1)}, u32[]{:S(2)}) copy-start(bf16[512,128]{1,0:T(8,128)(2,1)} %radial_in.1) | copy-start | bytes 393220
  1.5 28.9 %copy-start.1 = (s32[64,128]{1,0:T(8,128)S(1)}, s32[64,128]{1,0:T(8,128)}, u32[]{:S(2)}) copy-start(s32[64,128]{1,0:T(8,128)} %slots.3) | copy-start | bytes 98308
  1.5 9.7 %collective-permute-start = (bf16[64,640]{1,0:T(8,128)(2,1)S(1)}, bf16[64,640]{1,0:T(8,128)(2,1)S(1)}, u32[]{:S(2)}, u32[]{:S(2)}) collective-permute-start(bf16[64,640]{1,0:T(8,128)(2,1)S(1)} %shard_map.104.here_shard), channel_id=1, source_target_pairs={{0,1},{1,0},{2,3},{3,2},{4,5},{5,4},{6,7},{7,6},{8,9},{9,8},{10,11... | collective-permute-start | bytes 245768 | tf_op jit(solution)/shard_map/ppermute | solution.py:349
  24.2 8.6 %collective-permute-start.1 = (bf16[4,128,640]{2,1,0:T(8,128)(2,1)S(1)}, bf16[4,128,640]{2,1,0:T(8,128)(2,1)S(1)}, u32[]{:S(2)}, u32[]{:S(2)}) collective-permute-start(bf16[4,128,640]{2,1,0:T(8,128)(2,1)S(1)} %all_to_all.15.gathered.own), channel_id=1, source_target_pairs={{0,8},{8,0},{16,24},{24,16},{32,40},{40,32},{48,56},{56,48},{64,72... | collective-permute-start | bytes 1966088 | tf_op jit(solution)/shard_map/ppermute | solution.py:361
  27.4 1.7 %collective-permute-start.3 = (f32[3,128]{1,0:T(4,128)S(1)}, f32[3,128]{1,0:T(4,128)S(1)}, u32[]{:S(2)}, u32[]{:S(2)}) collective-permute-start(f32[3,128]{1,0:T(4,128)S(1)} %copy-done.3), channel_id=1, source_target_pairs={{0,8},{8,0},{16,24},{24,16},{32,40},{40,32},{48,56},{56,48},{64,72... | collective-permute-start | bytes 4616 | tf_op jit(solution)/shard_map/ppermute | solution.py:352
  27.4 3.0 %collective-permute-start.4 = (f32[3,128]{1,0:T(4,128)S(1)}, f32[3,128]{1,0:T(4,128)S(1)}, u32[]{:S(2)}, u32[]{:S(2)}) collective-permute-start(f32[3,128]{1,0:T(4,128)S(1)} %copy-done.3), channel_id=1, source_target_pairs={{8,16},{16,8},{9,17},{17,9},{10,18},{18,10},{11,19},{19,11},{12,20... | collective-permute-start | bytes 4616 | tf_op jit(solution)/shard_map/ppermute | solution.py:353
  31.5 4.5 %collective-permute-start.2 = (bf16[4,128,128]{2,1,0:T(8,128)(2,1)S(1)}, bf16[4,128,128]{2,1,0:T(8,128)(2,1)S(1)}, u32[]{:S(2)}, u32[]{:S(2)}) collective-permute-start(bf16[4,128,128]{2,1,0:T(8,128)(2,1)S(1)} %slice.4), channel_id=1, source_target_pairs={{8,16},{16,8},{9,17},{17,9},{10,18},{18,10},{11,19},{19,11},{12,20... | collective-permute-start | bytes 393224 | tf_op jit(solution)/shard_map/ppermute | solution.py:360
  32.7 3.3 %copy-start.2 = (s32[64,128]{1,0:T(8,128)S(1)}, s32[64,128]{1,0:T(8,128)}, u32[]{:S(2)}) copy-start(s32[64,128]{1,0:T(8,128)} %valid.1) | copy-start | bytes 98308
  32.8 3.3 %copy-start.4 = (f32[512]{0:T(512)S(1)}, f32[512]{0:T(512)}, u32[]{:S(2)}) copy-start(f32[512]{0:T(512)} %param.17) | copy-start | bytes 6148
  32.8 3.3 %copy-start.5 = (s32[128]{0:T(128)S(1)}, s32[128]{0:T(128)}, u32[]{:S(2)}) copy-start(s32[128]{0:T(128)} %param.11) | copy-start | bytes 1540
